TPU v7x, 256 devices: a whole 4x4x8 slice. The times are simulated.
256 devices in a mesh: band: 64 (over x, y, z_hi, core), chan: 4 (over z_lo).
Axes of the slice: x: 4, y: 4, z: 8 (z_hi: 2, z_lo: 4; z = z_hi * 4 + z_lo), core: 2. Of those that a mesh axis runs over, the one named last changes fastest.
Arguments:
- cells_next: bfloat16 [131072, 1024], P('band', 'chan'), may hold values from -6 to 6
- node_embed: bfloat16 [16384, 1024], P('band', 'chan'), may hold values from -6 to 6
- enc_mix: bfloat16 [1024, 1024], P(None, 'chan'), may hold values from -0.1875 to 0.1875
- out_cotangent: bfloat16 [131072, 1024], P('band', 'chan'), may hold values from -16 to 16
- decoded_saved: bfloat16 [131072, 1024], P('band', 'chan'), may hold values from -6 to 6
- dec_proj: bfloat16 [1024, 1024], P(None, 'chan'), may hold values from -0.1875 to 0.1875
- tile_source: int32 [128, 16], replicated, may hold values from 0 to 1023, as said below
- tile_codes: int32 [128, 16, 128, 128], P('band'), may hold values from 0 to 65535
Outputs:
- hidden_nodes: bfloat16 [16384, 1024], P('band', 'chan')
- node_grad: bfloat16 [16384, 1024], P('band', 'chan')
- w_dec_grad: float32 [1024, 1024], P('band', 'chan')
Inputs may be any that keep to these rules, and one draw needn't show every extreme that they name: `tile_source`: each entry is a cell block; cell block c lies in band c // 16 and node block n in band n // 2. The cell blocks of a node block's tiles lie within 3 bands of its own. Of the 32 tiles of one band's node blocks, exactly 8 read that band itself and at most 8 read any other one band.
All inputs are finite; a program needn't handle non-finite values.
Results may differ from a plain program's by a relative error of at most 0.0049.
Values may be sent and summed in bfloat16 or wider, within the bound.
A program may use at most 64 MiB of HBM per device.

v0:
```python
import jax
import jax.numpy as jnp
from jax import lax
from jax.sharding import PartitionSpec as P

BLK = 128
K = 16
R = 3
CB_DEV = 16
NB_DEV = 2
CAP = 8


def shifted(x, axis, by):
    peers = lax.axis_size(axis)
    pairs = [(i, i + by) for i in range(peers) if 0 <= i + by < peers]
    return lax.ppermute(x, axis, pairs)


def sent_to_all(x, axis):
    copies = jnp.broadcast_to(x, (lax.axis_size(axis), *x.shape))
    return lax.all_to_all(copies, axis, split_axis=0, concat_axis=0, tiled=True)


def joined_along(blocks, dim):
    shape = list(blocks.shape[1:])
    shape[dim] *= blocks.shape[0]
    return jnp.moveaxis(blocks, 0, dim).reshape(shape)


def collect(x, axis, dim):
    blocks = sent_to_all(x, axis)
    return joined_along(blocks, dim)


def split_up(x, dim, peers):
    shape = x.shape
    blocks = x.reshape(*shape[:dim], peers, shape[dim] // peers, *shape[dim + 1 :])
    return jnp.moveaxis(blocks, dim, 0)


def sent_and_summed(x, axis, dim):
    peers = lax.axis_size(axis)
    blocks = lax.all_to_all(split_up(x, dim, peers), axis, 0, 0, tiled=True)
    return jnp.sum(blocks.astype(jnp.float32), axis=0)


def split_codes(code_words):
    low_codes = (code_words % 256 - 128).astype(jnp.bfloat16)
    high_codes = (code_words // 256 - 128).astype(jnp.bfloat16)
    return (low_codes, high_codes)


def plan_for(tile_source, owner_band):
    source_rows = lax.dynamic_slice_in_dim(tile_source, owner_band * NB_DEV, NB_DEV, 0).reshape(-1)
    source_band = source_rows // CB_DEV
    local_block = source_rows % CB_DEV
    offset = source_band - owner_band + R
    markers = (offset[:, None] == jnp.arange(2 * R + 1, dtype=jnp.int32)[None, :]).astype(jnp.int32)
    earlier = jnp.cumsum(markers, axis=0) - markers
    slot_index = jnp.sum(earlier * markers, axis=1)
    return (offset, slot_index, local_block)


def send_tables(tile_source, my_band, band_count):
    tables = {}
    for shift_by in range(-R, R + 1):
        if shift_by != 0:
            target = jnp.clip(my_band + shift_by, 0, band_count - 1)
            offset, slot_index, local_block = plan_for(tile_source, target)
            chosen = (offset[:, None] == R - shift_by) & (
                slot_index[:, None] == jnp.arange(CAP, dtype=jnp.int32)[None, :]
            )
            tables[shift_by] = jnp.sum(jnp.where(chosen, local_block[:, None], 0), axis=0)
    return tables


def pull_slots(blocks, tables, offset, slot_index, local_block, sender):
    pieces = []
    starts = []
    filled = 0
    for position in range(2 * R + 1):
        shift_by = R - position
        starts.append(filled)
        if shift_by == 0:
            pieces.append(blocks)
            filled = filled + blocks.shape[0]
        else:
            pieces.append(sender(blocks[tables[shift_by]], shift_by))
            filled = filled + CAP
    pooled = jnp.concatenate(pieces, axis=0)
    start_table = jnp.array(starts, dtype=jnp.int32)
    matches = offset[:, None] == jnp.arange(2 * R + 1, dtype=jnp.int32)[None, :]
    base_index = jnp.sum(jnp.where(matches, start_table[None, :], 0), axis=1)
    within = jnp.where(offset == R, local_block, slot_index)
    return pooled[base_index + within]


def shards(
    cells_next, node_embed, enc_mix, out_cotangent, decoded_saved, dec_proj, tile_source, tile_codes
):
    band_count = lax.axis_size("band")
    my_band = lax.axis_index("band")
    tile_scale = (3.0 / (K * BLK)) ** 0.5 / 128.0
    channels = cells_next.shape[1]
    offset, slot_index, local_block = plan_for(tile_source, my_band)
    enc_tile, dec_tile = split_codes(tile_codes)
    cell_blocks = cells_next.reshape(CB_DEV, BLK, channels)

    def send_cells_slot(shard_piece, shift_by):
        return shifted(shard_piece, "band", shift_by)

    def send_grads_slot(shard_piece, shift_by):
        return shifted(shard_piece, "band", shift_by)

    tables = send_tables(tile_source, my_band, band_count)
    cell_pieces = pull_slots(cell_blocks, tables, offset, slot_index, local_block, send_cells_slot)
    whole_grad = lax.all_gather(out_cotangent, "chan", axis=1, tiled=True)
    cell_grad = jnp.dot(whole_grad, dec_proj, preferred_element_type=jnp.float32).astype(
        jnp.bfloat16
    )
    grad_blocks = cell_grad.reshape(CB_DEV, BLK, channels)
    grad_pieces = pull_slots(grad_blocks, tables, offset, slot_index, local_block, send_grads_slot)

    def combine(tile_set, gathered):
        arranged = gathered.reshape(NB_DEV, K, BLK, channels)
        summed = jnp.einsum(
            "nkab,nkbd->nad", tile_set, arranged, preferred_element_type=jnp.float32
        )
        return (summed * tile_scale).astype(jnp.bfloat16).reshape(NB_DEV * BLK, channels)

    aggregate = combine(enc_tile, cell_pieces)
    node_grad = combine(dec_tile, grad_pieces)
    mixed_rows = jnp.dot(collect(aggregate, "chan", 1), enc_mix, preferred_element_type=jnp.float32)
    hidden_nodes = (node_embed.astype(jnp.float32) + jax.nn.silu(mixed_rows)).astype(jnp.bfloat16)
    cells_total = cells_next.shape[0] * band_count
    w_dec_grad = sent_and_summed(
        lax.dot_general(
            whole_grad, decoded_saved, (((0,), (0,)), ((), ())), preferred_element_type=jnp.float32
        ).astype(jnp.bfloat16),
        "band",
        0,
    ) * cells_total ** (-0.5)
    return (hidden_nodes, node_grad, w_dec_grad)


def solution(mesh):
    in_specs = (
        P("band", "chan"),
        P("band", "chan"),
        P(None, "chan"),
        P("band", "chan"),
        P("band", "chan"),
        P(None, "chan"),
        P(),
        P("band", None, None, None),
    )
    out_specs = (P("band", "chan"), P("band", "chan"), P("band", "chan"))
    return jax.shard_map(shards, mesh=mesh, in_specs=in_specs, out_specs=out_specs, check_vma=False)
```

profile of v0, /device:TPU:32, one launch (start us, length us, event | category | flops | bytes accessed | tf_op | source)
XLA Modules:
  0.0 331.4 jit_solution(10718570485615570895)
XLA Ops:
  9.8 2.6 gather_fusion
  12.4 7.7 %collective-permute-start = (bf16[8,128,256]{2,1,0:T(8,128)(2,1)}, bf16[8,128,256]{2,1,0:T(8,128)(2,1)S(1)}, u32[]{:S(2)}, u32[]{:S(2)}) collective-permute-start(bf16[8,128,256]{2,1,0:T(8,128)(2,1)} %gather_fusion), channel_id=1, source_target_pairs={{0,12},{4,16},{8,20},{12,24},{16,28},{20,32},{24,36},{28,40},{32,4... | collective-permute-start | bytes 1572872 | tf_op jit(solution)/shard_map/ppermute | solution.py:17
  20.6 2.6 gather_fusion.1
  23.2 2.6 collective-permute-start.1
  26.6 2.6 gather_fusion.2
  29.2 4.0 %collective-permute-start.2 = (bf16[8,128,256]{2,1,0:T(8,128)(2,1)}, bf16[8,128,256]{2,1,0:T(8,128)(2,1)}, u32[]{:S(2)}, u32[]{:S(2)}) collective-permute-start(bf16[8,128,256]{2,1,0:T(8,128)(2,1)} %gather_fusion.2), channel_id=1, source_target_pairs={{0,4},{4,8},{8,12},{12,16},{16,20},{20,24},{24,28},{28,32},{32,36}... | collective-permute-start | bytes 1572872 | tf_op jit(solution)/shard_map/ppermute | solution.py:17
  42.3 19.4 %collective-permute-done = bf16[8,128,256]{2,1,0:T(8,128)(2,1)S(1)} collective-permute-done((bf16[8,128,256]{2,1,0:T(8,128)(2,1)}, bf16[8,128,256]{2,1,0:T(8,128)(2,1)S(1)}, u32[]{:S(2)}, u32[]{:S(2)}) %collective-permute-start) | collective-permute-done | bytes 524320 | tf_op jit(solution)/shard_map/ppermute | solution.py:17
  63.8 35.1 %collective-permute-done.1 = bf16[8,128,256]{2,1,0:T(8,128)(2,1)S(1)} collective-permute-done((bf16[8,128,256]{2,1,0:T(8,128)(2,1)}, bf16[8,128,256]{2,1,0:T(8,128)(2,1)S(1)}, u32[]{:S(2)}, u32[]{:S(2)}) %collective-permute-start.1) | collective-permute-done | bytes 524320 | tf_op jit(solution)/shard_map/ppermute | solution.py:17
  104.6 69.7 %collective-permute-done.4 = bf16[8,128,256]{2,1,0:T(8,128)(2,1)} collective-permute-done((bf16[8,128,256]{2,1,0:T(8,128)(2,1)}, bf16[8,128,256]{2,1,0:T(8,128)(2,1)}, u32[]{:S(2)}, u32[]{:S(2)}) %collective-permute-start.4) | collective-permute-done | bytes 524320 | tf_op jit(solution)/shard_map/ppermute | solution.py:17
  176.2 3.5 %collective-permute-done.5 = bf16[8,128,256]{2,1,0:T(8,128)(2,1)S(1)} collective-permute-done((bf16[8,128,256]{2,1,0:T(8,128)(2,1)}, bf16[8,128,256]{2,1,0:T(8,128)(2,1)S(1)}, u32[]{:S(2)}, u32[]{:S(2)}) %collective-permute-start.5) | collective-permute-done | bytes 524320 | tf_op jit(solution)/shard_map/ppermute | solution.py:17
  180.6 2.9 gather_fusion.6
  183.5 2.6 fusion.8
  187.1 3.9 %all-to-all-start = ((bf16[4,256,256]{1,2,0:T(8,128)(2,1)}), bf16[4,256,256]{1,2,0:T(8,128)(2,1)S(1)}, u32[]{:S(2)}, u32[]{:S(2)}) async-start(bf16[4,256,256]{1,2,0:T(8,128)(2,1)} %broadcast_in_dim.68), calls=%async_computation | async-start | bytes 1048576 | tf_op jit(solution)/shard_map/all_to_all | solution.py:22
  191.0 3.6 %convolution_convert_fusion = bf16[2048,256]{1,0:T(8,128)(2,1)S(1)} fusion(bf16[2048,1024]{1,0:T(8,128)(2,1)} %all-gather.2.cloned.1.call-done, bf16[1024,256]{1,0:T(8,128)(2,1)} %param.15), kind=kOutput, calls=%fused_computation.19 | convolution fusion | flops 1074266112 | bytes 5767168 | tf_op jit(solution)/shard_map/dot_general | solution.py:119
  197.3 2.2 all-to-all-done
  199.5 2.1 add_convert_fusion
  208.5 8.4 %collective-permute-start.7 = (bf16[8,128,256]{2,1,0:T(8,128)(2,1)}, bf16[8,128,256]{2,1,0:T(8,128)(2,1)}, u32[]{:S(2)}, u32[]{:S(2)}) collective-permute-start(bf16[8,128,256]{2,1,0:T(8,128)(2,1)} %gather_fusion.8), channel_id=1, source_target_pairs={{0,8},{4,12},{8,16},{12,20},{16,24},{20,28},{24,32},{28,36},{32,40... | collective-permute-start | bytes 1572872 | tf_op jit(solution)/shard_map/ppermute | solution.py:17
  216.8 2.8 collective-permute-start.8
  222.2 4.3 %convolution_convert_fusion.1 = bf16[1024,256]{1,0:T(8,128)(2,1)} fusion(bf16[2048,1024]{1,0:T(8,128)(2,1)} %all-gather.2.cloned.1.call-done, bf16[2048,256]{1,0:T(8,128)(2,1)S(1)} %copy-done), kind=kOutput, calls=%fused_computation.27 | convolution fusion | flops 1074003968 | bytes 5767168 | tf_op jit(solution)/shard_map/dot_general | solution.py:138
  226.6 22.4 %all-to-all-start.1 = ((bf16[64,16,256]{2,1,0:T(8,128)(2,1)}), bf16[64,16,256]{2,1,0:T(8,128)(2,1)}, u32[]{:S(2)}, u32[]{:S(2)}) async-start(bf16[64,16,256]{2,1,0:T(8,128)(2,1)} %bitcast.27), calls=%async_computation.1 | async-start | bytes 1048576 | tf_op jit(solution)/shard_map/all_to_all | solution.py:44
  257.8 48.0 %collective-permute-done.10 = bf16[8,128,256]{2,1,0:T(8,128)(2,1)S(1)} collective-permute-done((bf16[8,128,256]{2,1,0:T(8,128)(2,1)}, bf16[8,128,256]{2,1,0:T(8,128)(2,1)S(1)}, u32[]{:S(2)}, u32[]{:S(2)}) %collective-permute-start.10) | collective-permute-done | bytes 524320 | tf_op jit(solution)/shard_map/ppermute | solution.py:17
  306.6 8.8 %collective-permute-done.11 = bf16[8,128,256]{2,1,0:T(8,128)(2,1)S(1)} collective-permute-done((bf16[8,128,256]{2,1,0:T(8,128)(2,1)}, bf16[8,128,256]{2,1,0:T(8,128)(2,1)S(1)}, u32[]{:S(2)}, u32[]{:S(2)}) %collective-permute-start.11) | collective-permute-done | bytes 524320 | tf_op jit(solution)/shard_map/ppermute | solution.py:17
  316.3 2.9 gather_fusion.13
  319.1 3.7 %fusion.9 = bf16[2,128,256]{2,1,0:T(8,128)(2,1)} fusion(bf16[2,16,128,256]{3,2,1,0:T(8,128)(2,1)S(1)} %bitcast.80, s32[2,16,128,128]{3,2,1,0:T(8,128)} %param.17), kind=kOutput, calls=%fused_computation.33 | convolution fusion | flops 277479424 | bytes 4325376 | tf_op jit(solution)/shard_map/nkab,nkbd->nad/dot_general | solution.py:127
  (116 shorter events, 48.8 us)
Async XLA Ops:
  7.2 215.1 %copy-start = (bf16[2048,256]{1,0:T(8,128)(2,1)S(1)}, bf16[2048,256]{1,0:T(8,128)(2,1)}, u32[]{:S(2)}) copy-start(bf16[2048,256]{1,0:T(8,128)(2,1)} %param.14) | copy-start | bytes 3145732
  7.2 33.4 %copy-start.2 = (s32[7]{0:T(128)S(1)}, s32[7]{0:T(128)}, u32[]{:S(2)}) copy-start(s32[7]{0:T(128)} %constant.191.clone) | copy-start | bytes 88
  7.2 26.5 %copy-start.1 = (bf16[2048,256]{1,0:T(8,128)(2,1)S(1)}, bf16[2048,256]{1,0:T(8,128)(2,1)}, u32[]{:S(2)}) copy-start(bf16[2048,256]{1,0:T(8,128)(2,1)} %param.10) | copy-start | bytes 3145732
  7.2 183.8 %all-gather.2.cloned.1.call-start = ((), (), s32[]{:S(2)}) async-start(), calls=%async_computation.2 | async-start | bytes 5242880 | tf_op jit(solution)/shard_map/all_gather | solution.py:118
  12.4 49.3 %collective-permute-start = (bf16[8,128,256]{2,1,0:T(8,128)(2,1)}, bf16[8,128,256]{2,1,0:T(8,128)(2,1)S(1)}, u32[]{:S(2)}, u32[]{:S(2)}) collective-permute-start(bf16[8,128,256]{2,1,0:T(8,128)(2,1)} %gather_fusion), channel_id=1, source_target_pairs={{0,12},{4,16},{8,20},{12,24},{16,28},{20,32},{24,36},{28,40},{32,4... | collective-permute-start | bytes 1572872 | tf_op jit(solution)/shard_map/ppermute | solution.py:17
  23.2 75.7 %collective-permute-start.1 = (bf16[8,128,256]{2,1,0:T(8,128)(2,1)}, bf16[8,128,256]{2,1,0:T(8,128)(2,1)S(1)}, u32[]{:S(2)}, u32[]{:S(2)}) collective-permute-start(bf16[8,128,256]{2,1,0:T(8,128)(2,1)} %gather_fusion.1), channel_id=1, source_target_pairs={{0,8},{4,12},{8,16},{12,20},{16,24},{20,28},{24,32},{28,36},{32,40... | collective-permute-start | bytes 1572872 | tf_op jit(solution)/shard_map/ppermute | solution.py:17
  29.2 70.6 %collective-permute-start.2 = (bf16[8,128,256]{2,1,0:T(8,128)(2,1)}, bf16[8,128,256]{2,1,0:T(8,128)(2,1)}, u32[]{:S(2)}, u32[]{:S(2)}) collective-permute-start(bf16[8,128,256]{2,1,0:T(8,128)(2,1)} %gather_fusion.2), channel_id=1, source_target_pairs={{0,4},{4,8},{8,12},{12,16},{16,20},{20,24},{24,28},{28,32},{32,36}... | collective-permute-start | bytes 1572872 | tf_op jit(solution)/shard_map/ppermute | solution.py:17
  35.1 67.6 %collective-permute-start.3 = (bf16[8,128,256]{2,1,0:T(8,128)(2,1)}, bf16[8,128,256]{2,1,0:T(8,128)(2,1)}, u32[]{:S(2)}, u32[]{:S(2)}) collective-permute-start(bf16[8,128,256]{2,1,0:T(8,128)(2,1)} %gather_fusion.3), channel_id=1, source_target_pairs={{4,0},{8,4},{12,8},{16,12},{20,16},{24,20},{28,24},{32,28},{36,32}... | collective-permute-start | bytes 1572872 | tf_op jit(solution)/shard_map/ppermute | solution.py:17
  38.6 135.8 %collective-permute-start.4 = (bf16[8,128,256]{2,1,0:T(8,128)(2,1)}, bf16[8,128,256]{2,1,0:T(8,128)(2,1)}, u32[]{:S(2)}, u32[]{:S(2)}) collective-permute-start(bf16[8,128,256]{2,1,0:T(8,128)(2,1)} %gather_fusion.4), channel_id=1, source_target_pairs={{8,0},{12,4},{16,8},{20,12},{24,16},{28,20},{32,24},{36,28},{40,32... | collective-permute-start | bytes 1572872 | tf_op jit(solution)/shard_map/ppermute | solution.py:17
  61.7 118.0 %collective-permute-start.5 = (bf16[8,128,256]{2,1,0:T(8,128)(2,1)}, bf16[8,128,256]{2,1,0:T(8,128)(2,1)S(1)}, u32[]{:S(2)}, u32[]{:S(2)}) collective-permute-start(bf16[8,128,256]{2,1,0:T(8,128)(2,1)} %gather_fusion.5), channel_id=1, source_target_pairs={{12,0},{16,4},{20,8},{24,12},{28,16},{32,20},{36,24},{40,28},{44,3... | collective-permute-start | bytes 1572872 | tf_op jit(solution)/shard_map/ppermute | solution.py:17
  187.1 12.4 %all-to-all-start = ((bf16[4,256,256]{1,2,0:T(8,128)(2,1)}), bf16[4,256,256]{1,2,0:T(8,128)(2,1)S(1)}, u32[]{:S(2)}, u32[]{:S(2)}) async-start(bf16[4,256,256]{1,2,0:T(8,128)(2,1)} %broadcast_in_dim.68), calls=%async_computation | async-start | bytes 1048576 | tf_op jit(solution)/shard_map/all_to_all | solution.py:22
  191.0 8.5 %copy-start.3 = (bf16[256,256]{1,0:T(8,128)(2,1)S(1)}, bf16[256,256]{1,0:T(8,128)(2,1)}, u32[]{:S(2)}) copy-start(bf16[256,256]{1,0:T(8,128)(2,1)} %param.11) | copy-start | bytes 393220
  196.0 53.0 %collective-permute-start.6 = (bf16[8,128,256]{2,1,0:T(8,128)(2,1)}, bf16[8,128,256]{2,1,0:T(8,128)(2,1)S(1)}, u32[]{:S(2)}, u32[]{:S(2)}) collective-permute-start(bf16[8,128,256]{2,1,0:T(8,128)(2,1)} %gather_fusion.7), channel_id=1, source_target_pairs={{0,12},{4,16},{8,20},{12,24},{16,28},{20,32},{24,36},{28,40},{32,4... | collective-permute-start | bytes 1572872 | tf_op jit(solution)/shard_map/ppermute | solution.py:17
  208.5 42.7 %collective-permute-start.7 = (bf16[8,128,256]{2,1,0:T(8,128)(2,1)}, bf16[8,128,256]{2,1,0:T(8,128)(2,1)}, u32[]{:S(2)}, u32[]{:S(2)}) collective-permute-start(bf16[8,128,256]{2,1,0:T(8,128)(2,1)} %gather_fusion.8), channel_id=1, source_target_pairs={{0,8},{4,12},{8,16},{12,20},{16,24},{20,28},{24,32},{28,36},{32,40... | collective-permute-start | bytes 1572872 | tf_op jit(solution)/shard_map/ppermute | solution.py:17
  216.8 36.2 %collective-permute-start.8 = (bf16[8,128,256]{2,1,0:T(8,128)(2,1)}, bf16[8,128,256]{2,1,0:T(8,128)(2,1)}, u32[]{:S(2)}, u32[]{:S(2)}) collective-permute-start(bf16[8,128,256]{2,1,0:T(8,128)(2,1)} %gather_fusion.9), channel_id=1, source_target_pairs={{0,4},{4,8},{8,12},{12,16},{16,20},{20,24},{24,28},{28,32},{32,36}... | collective-permute-start | bytes 1572872 | tf_op jit(solution)/shard_map/ppermute | solution.py:17
  219.6 36.3 %collective-permute-start.9 = (bf16[8,128,256]{2,1,0:T(8,128)(2,1)}, bf16[8,128,256]{2,1,0:T(8,128)(2,1)}, u32[]{:S(2)}, u32[]{:S(2)}) collective-permute-start(bf16[8,128,256]{2,1,0:T(8,128)(2,1)} %gather_fusion.10), channel_id=1, source_target_pairs={{4,0},{8,4},{12,8},{16,12},{20,16},{24,20},{28,24},{32,28},{36,32}... | collective-permute-start | bytes 1572872 | tf_op jit(solution)/shard_map/ppermute | solution.py:17
  220.9 84.9 %collective-permute-start.10 = (bf16[8,128,256]{2,1,0:T(8,128)(2,1)}, bf16[8,128,256]{2,1,0:T(8,128)(2,1)S(1)}, u32[]{:S(2)}, u32[]{:S(2)}) collective-permute-start(bf16[8,128,256]{2,1,0:T(8,128)(2,1)} %gather_fusion.11), channel_id=1, source_target_pairs={{8,0},{12,4},{16,8},{20,12},{24,16},{28,20},{32,24},{36,28},{40,32... | collective-permute-start | bytes 1572872 | tf_op jit(solution)/shard_map/ppermute | solution.py:17
  226.6 96.3 %all-to-all-start.1 = ((bf16[64,16,256]{2,1,0:T(8,128)(2,1)}), bf16[64,16,256]{2,1,0:T(8,128)(2,1)}, u32[]{:S(2)}, u32[]{:S(2)}) async-start(bf16[64,16,256]{2,1,0:T(8,128)(2,1)} %bitcast.27), calls=%async_computation.1 | async-start | bytes 1048576 | tf_op jit(solution)/shard_map/all_to_all | solution.py:44
  249.0 66.4 %collective-permute-start.11 = (bf16[8,128,256]{2,1,0:T(8,128)(2,1)}, bf16[8,128,256]{2,1,0:T(8,128)(2,1)S(1)}, u32[]{:S(2)}, u32[]{:S(2)}) collective-permute-start(bf16[8,128,256]{2,1,0:T(8,128)(2,1)} %gather_fusion.12), channel_id=1, source_target_pairs={{12,0},{16,4},{20,8},{24,12},{28,16},{32,20},{36,24},{40,28},{44,3... | collective-permute-start | bytes 1572872 | tf_op jit(solution)/shard_map/ppermute | solution.py:17
Sparse Core Ops, SparseCore 0:
  9.8 133.9 all-gather.1
where the time goes:
time: 333 us; the launch traced here: 331 us
  waiting for transfers between devices  187 us (56%)
  starting transfers between devices  60.8 us (18%)
  local copies, waits for them, and re-layouts  47.7 us (14%)
  matrix products  16.3 us (5%)
  between operations  14.4 us (4%)
  other arithmetic  4.84 us (1%)
    ppermute x12, waiting for transfers between devices, shifted(): return lax.ppermute(x, axis, pairs)  184 us
    ppermute x12, starting transfers between devices, shifted(): return lax.ppermute(x, axis, pairs)  34.4 us
    all_to_all x1, starting transfers between devices, sent_and_summed(): blocks = lax.all_to_all(split_up(x, dim, peers), axis, 0, 0, tiled=True)  22.4 us
    gather x12, local copies, waits for them, and re-layouts, pull_slots(): pieces.append(sender(blocks[tables[shift_by]], shift_by))  20.4 us
    unnamed x20, local copies, waits for them, and re-layouts  16.8 us
  transfers between devices with their start and end apart: 15, of which 7 were waited for; matrix products, arithmetic and copies ran while one was open for 20% of the time, Pallas kernels for 0%

commit v1 on v0

v1 whole, which is shorter than its diff:
```python
import jax
import jax.numpy as jnp
from jax import lax
from jax.experimental import pallas as pl
from jax.experimental.pallas import tpu as pltpu
from jax.sharding import PartitionSpec as P

BLK = 128
K = 16
NB_DEV = 2
CHIPS = 32
TILES = NB_DEV * K
SLOTS = 16
T2 = 8
CH = 256
ROWS = 2048
QROWS = 512
NODES = 256
SCALE = (3.0 / (K * BLK)) ** 0.5 / 128.0
MESH = pl.DeviceIdType.MESH
BF = jnp.bfloat16
F32 = jnp.float32

UP = (0, 4, 16, 20)
DOWN = (8, 12, 24, 28)
CHUNK = 4


def chip_links(chip, z_hi, core):
    side = 1 - 2 * z_hi
    across = chip + side
    beyond = (chip - side + CHIPS) % CHIPS
    relay_to = (chip + 2 * side + CHIPS) % CHIPS
    two_to = (chip + 4 * core - 2 + CHIPS) % CHIPS
    two_from = (chip - 4 * core + 2 + CHIPS) % CHIPS
    return across, beyond, relay_to, two_to, two_from


def slot_tables(tile_source, my_band):
    chip, core = my_band // 2, my_band % 2
    across, beyond, _, two_to, two_from = chip_links(chip, chip % 2, core)
    targets = jnp.stack(
        [my_band] * 4 + [2 * beyond + core, 2 * across + core, 2 * two_from + core, my_band]
    )
    sources = jnp.stack([beyond, across, two_to, chip, chip, chip, chip, chip])
    blocks = tile_source.reshape(-1, TILES)[targets]
    tile = jnp.arange(TILES, dtype=jnp.int32)
    match = (blocks // 32) == sources[:, None]
    before = tile[None, :, None] > tile[None, None, :]
    rank = jnp.sum((match[:, None, :] & before).astype(jnp.int32), axis=2)
    sending = (jnp.arange(8) < 4)[:, None]
    entry = jnp.where(sending, tile[None, :] + 256, blocks % 32 + 256 * (tile[None, :] // K))
    slot = jnp.arange(SLOTS, dtype=jnp.int32)
    chosen = match[:, :, None] & (rank[:, :, None] == slot[None, None, :])
    return jnp.sum(jnp.where(chosen, entry[:, :, None], 0), axis=1)


def kernel(
    table,
    cells_hbm,
    embed_hbm,
    mix_hbm,
    cot_hbm,
    saved_hbm,
    proj_hbm,
    codes_hbm,
    hidden_out,
    grad_out,
    w_out,
    codes,
    cells,
    cot,
    cot_all,
    saved_all,
    mix,
    proj,
    embed,
    packed,
    own_packed,
    got_z,
    got_y,
    got_two,
    lhs,
    rhs,
    own_sum,
    part_send,
    part_recv,
    agg_all,
    w_part,
    core_recv,
    y_own,
    y_send,
    y_recv,
    x_send,
    x_recv,
    z_send,
    z_recv,
    load_sem,
    share_send,
    share_recv,
    up_send,
    up_recv,
    down_send,
    down_recv,
    relay_send,
    relay_recv,
    two_send,
    two_recv,
    a_send,
    a_recv,
    core_send_sem,
    core_recv_sem,
    y_send_sem,
    y_recv_sem,
    x_send_sem,
    x_recv_sem,
    z_send_sem,
    z_recv_sem,
    part_send_sem,
    part_recv_sem,
    agg_send_sem,
    agg_recv_sem,
):
    band = lax.axis_index("band")
    q = lax.axis_index("chan")
    core = band % 2
    chip = band // 2
    h = chip % 2
    y = (band // 4) % 4
    x = band // 16
    across, beyond, relay_to, two_to, two_from = chip_links(chip, h, core)

    def at_chip(other_chip, chan):
        return (2 * other_chip + core, chan)

    def remote(src, dst, send, recv, device):
        return pltpu.make_async_remote_copy(
            src_ref=src,
            dst_ref=dst,
            send_sem=send,
            recv_sem=recv,
            device_id=device,
            device_id_type=MESH,
        )

    sibling = (band + 1 - 2 * core, q)
    across_q = [at_chip(across, (q + d) % 4) for d in range(4)]
    along_q = [(band, (q + d) % 4) for d in range(1, 4)]
    along_y = [(x * 16 + ((y + d) % 4) * 4 + h * 2 + core, q) for d in range(1, 4)]
    along_x = [(((x + d) % 4) * 16 + y * 4 + h * 2 + core, q) for d in range(1, 4)]

    barrier = pltpu.get_barrier_semaphore()
    partners = (
        [sibling]
        + across_q
        + along_q
        + along_y
        + along_x
        + [at_chip(two_to, q), at_chip(two_from, q), at_chip(beyond, q)]
    )
    for partner in partners:
        pl.semaphore_signal(barrier, inc=1, device_id=partner, device_id_type=MESH)

    loads = [
        pltpu.make_async_copy(codes_hbm, codes, load_sem.at[0]),
        pltpu.make_async_copy(cells_hbm, cells.at[core], load_sem.at[1]),
        pltpu.make_async_copy(cot_hbm, cot.at[core], load_sem.at[2]),
        pltpu.make_async_copy(cot_hbm.at[q], cot_all.at[q], load_sem.at[3]),
        pltpu.make_async_copy(saved_hbm.at[q], saved_all.at[q], load_sem.at[4]),
        pltpu.make_async_copy(mix_hbm, mix, load_sem.at[5]),
        pltpu.make_async_copy(proj_hbm, proj, load_sem.at[6]),
        pltpu.make_async_copy(embed_hbm, embed, load_sem.at[7]),
    ]
    for load in loads:
        load.start()

    def pack(row, count, dest, base):
        def one(s, carry):
            item = table[row, s]
            words = codes[item & 31]
            low = ((words & 255) - 128).astype(F32)
            high = ((words >> 8) - 128).astype(F32)
            keep = jnp.where(item >= 256, 1.0, 0.0).astype(F32)
            dest[base + s, 0] = (low * keep).astype(BF)
            dest[base + s, 1] = (high * keep).astype(BF)
            return carry

        lax.fori_loop(0, count, one, 0)

    loads[0].wait()
    pack(0, SLOTS, packed, 0)
    pack(1, SLOTS, packed, 16)
    pack(2, T2, packed, 32)
    pl.semaphore_wait(barrier, len(partners))

    z_up = at_chip(jnp.where(q == 3, across, chip), (q + 1) % 4)
    z_down = at_chip(jnp.where(q == 0, across, chip), (q + 3) % 4)

    def up_copy(step, src):
        part = pl.ds(UP[step], CHUNK)
        return remote(src.at[part], got_z.at[part], up_send.at[step], up_recv.at[step], z_up)

    def down_copy(step, src):
        part = pl.ds(DOWN[step], CHUNK)
        return remote(src.at[part], got_z.at[part], down_send.at[step], down_recv.at[step], z_down)

    def relay_copy(index, start):
        part = pl.ds(start, CHUNK)
        return remote(
            got_z.at[part],
            got_y.at[part],
            relay_send.at[index],
            relay_recv.at[index],
            at_chip(relay_to, q),
        )

    relays = [
        relay_copy(index, start)
        for index, start in enumerate((UP[0], DOWN[0], UP[1], DOWN[1]))
    ]
    for step in range(4):

        @pl.when(q == 3)
        def _(step=step):
            up_copy(step, packed).start()

        @pl.when(q == 0)
        def _(step=step):
            down_copy(step, packed).start()

    two = remote(packed.at[pl.ds(32, T2)], got_two, two_send, two_recv, at_chip(two_to, q))
    two.start()
    shares = [
        remote(cells_hbm, cells.at[core], share_send.at[0], share_recv.at[0], sibling),
        remote(cot_hbm, cot.at[core], share_send.at[1], share_recv.at[1], sibling),
    ]
    for share in shares:
        share.start()

    a_copies = []
    for d in range(1, 4):
        other = (q + d) % 4
        for array, (src, dst) in enumerate(((cot_hbm, cot_all), (saved_hbm, saved_all))):
            index = 2 * (d - 1) + array
            a_copies.append(
                remote(src.at[other], dst.at[q], a_send.at[index], a_recv.at[index], (band, other))
            )
    waiting = list(a_copies)

    for step in range(4):
        up_copy(step, got_z).wait_recv()

        @pl.when(q < 3)
        def _(step=step):
            up_copy(step, got_z).start()

        down_copy(step, got_z).wait_recv()

        @pl.when(q > 0)
        def _(step=step):
            down_copy(step, got_z).start()

        if step < 2:
            relays[2 * step].start()
            relays[2 * step + 1].start()
        for _ in range(1 if step < 2 else 2):
            waiting.pop(0).start()

    def sums(row, count, tiles, base):
        def one(s, carry):
            item = table[row, s]
            column = pl.ds(pl.multiple_of(s * BLK, BLK), BLK)
            first = jnp.where(item < 256, 1.0, 0.0).astype(BF)
            second = jnp.where(item < 256, 0.0, 1.0).astype(BF)
            for which in range(2):
                tile = tiles[base + s, which]
                lhs[which, pl.ds(0, BLK), column] = tile * first
                lhs[which, pl.ds(BLK, BLK), column] = tile * second
            block = item & 31
            rhs[0, column, :] = cells[block // 16, (block // 4) % 4, block % 4]
            rhs[1, column, :] = cot[block // 16, (block // 4) % 4, block % 4]
            return carry

        lax.fori_loop(0, count, one, 0)
        depth = count * BLK
        return [
            jnp.dot(
                lhs[which, :, pl.ds(0, depth)],
                rhs[which, pl.ds(0, depth), :],
                preferred_element_type=F32,
            )
            for which in range(2)
        ]

    for load in loads[1:3]:
        load.wait()
    for share in shares:
        share.wait_recv()

    part_to = [at_chip(across, q), at_chip(two_from, q), at_chip(beyond, q)]
    part_copies = [
        remote(
            part_send.at[g], part_recv.at[g], part_send_sem.at[g], part_recv_sem.at[g], part_to[g]
        )
        for g in range(3)
    ]

    def send_part(g, row, count, tiles, base):
        result = sums(row, count, tiles, base)
        for which in range(2):
            part_send[g, which] = result[which].astype(BF)
        part_copies[g].start()

    send_part(0, 5, SLOTS, got_z, 16)
    two.wait_recv()
    send_part(1, 6, T2, got_two, 0)
    for copy in relays:
        copy.wait_recv()
    send_part(2, 4, SLOTS, got_y, 0)
    pack(3, SLOTS, own_packed, 0)
    result = sums(7, SLOTS, own_packed, 0)
    for which in range(2):
        own_sum[which] = result[which]

    for load in loads[3:5]:
        load.wait()
    for copy in a_copies:
        copy.wait_recv()

    core_copies = [
        remote(
            w_part.at[d, 1 - core],
            core_recv.at[d],
            core_send_sem.at[d],
            core_recv_sem.at[d],
            sibling,
        )
        for d in range(4)
    ]
    order = (1, 2, 3, 0)
    for d in order:
        left = cot_all.at[(x + d) % 4]

        def columns(j, carry, d=d, left=left):
            product = lax.dot_general(
                left[...].reshape(QROWS, CH),
                saved_all[j].reshape(QROWS, CH),
                (((0,), (0,)), ((), ())),
                preferred_element_type=F32,
            )
            span = pl.ds(pl.multiple_of(j * CH, CH), CH)
            for group in range(8):
                for half in range(2):
                    start = (2 * group + half) * 16
                    w_part[d, half, group // 2, pl.ds((group % 2) * 16, 16), span] = product[
                        start : start + 16
                    ]
            return carry

        lax.fori_loop(0, 4, columns, 0)
        core_copies[d].start()

    y_copies = {}
    for d in order:
        core_copies[d].wait_recv()
        for yy in range(4):
            total = w_part[d, core, yy] + core_recv[d, yy]
            y_own[d, yy] = total
            y_send[d, yy] = total.astype(BF)
        for e in range(1, 4):
            y_copies[d, e] = remote(
                y_send.at[d, (y + e) % 4],
                y_recv.at[d, e - 1],
                y_send_sem.at[d, e - 1],
                y_recv_sem.at[d, e - 1],
                along_y[e - 1],
            )
            y_copies[d, e].start()

    for copy in part_copies:
        copy.wait_recv()
    for which in range(2):
        total = own_sum[which]
        for g in range(3):
            total = total + part_recv[g, which].astype(F32)
        agg_all[q, which] = (total * SCALE).astype(BF)
    agg_copies = [
        remote(
            agg_all.at[q], agg_all.at[q], agg_send_sem.at[d], agg_recv_sem.at[d], along_q[d]
        )
        for d in range(3)
    ]
    for copy in agg_copies:
        copy.start()

    x_copies = {}
    for d in order:
        total = y_own[d, y]
        for e in range(1, 4):
            y_copies[d, e].wait_recv()
            total = total + y_recv[d, e - 1].astype(F32)
        if d > 0:
            x_send[d - 1] = total.astype(BF)
            x_copies[d] = remote(
                x_send.at[d - 1],
                x_recv.at[d - 1],
                x_send_sem.at[d - 1],
                x_recv_sem.at[d - 1],
                along_x[d - 1],
            )
            x_copies[d].start()
    for d in range(1, 4):
        x_copies[d].wait_recv()
        total = total + x_recv[d - 1].astype(F32)
    for hh in range(2):
        for qq in range(4):
            z_send[hh, qq] = total[hh * 16 : hh * 16 + 16, qq * CH : qq * CH + CH]
    z_copies = []
    for hd in range(2):
        for qd in range(4):
            if hd + qd > 0:
                index = hd * 4 + qd - 1
                chan = (q + qd) % 4
                device = at_chip(across, chan) if hd else (band, chan)
                to_h = 1 - h if hd else h
                z_copies.append(
                    remote(
                        z_send.at[to_h, chan],
                        z_recv.at[index],
                        z_send_sem.at[index],
                        z_recv_sem.at[index],
                        device,
                    )
                )
    for copy in z_copies:
        copy.start()

    for load in loads[5:8]:
        load.wait()
    for copy in agg_copies:
        copy.wait_recv()
    mixed = jnp.zeros((NODES, CH), F32)
    grad = jnp.zeros((NODES, CH), F32)
    for j in range(4):
        mixed = mixed + jnp.dot(
            agg_all[j, 0], mix[pl.ds(j * CH, CH), :], preferred_element_type=F32
        )
    hidden_out[...] = (embed[...].astype(F32) + mixed / (1.0 + jnp.exp(-mixed))).astype(BF)
    for j in range(4):
        grad = grad + jnp.dot(
            agg_all[j, 1], proj[pl.ds(j * CH, CH), :], preferred_element_type=F32
        )
    grad_out[...] = grad.astype(BF)

    total = z_send[h, q]
    for index, copy in enumerate(z_copies):
        copy.wait_recv()
        total = total + z_recv[index]
    w_out[...] = total * (ROWS * 64) ** (-0.5)

    for step in range(4):
        up_copy(step, got_z).wait_send()
        down_copy(step, got_z).wait_send()
    two.wait_send()
    ends = relays + shares + a_copies + part_copies + core_copies + agg_copies + z_copies
    for copy in ends + list(y_copies.values()) + list(x_copies.values()):
        copy.wait_send()


def shards(
    cells_next, node_embed, enc_mix, out_cotangent, decoded_saved, dec_proj, tile_source, tile_codes
):
    my_band = lax.axis_index("band")
    table = slot_tables(tile_source, my_band)
    hbm = pl.BlockSpec(memory_space=pl.ANY)
    vmem = pl.BlockSpec(memory_space=pltpu.VMEM)
    dma = pltpu.SemaphoreType.DMA
    scratch = [
        pltpu.VMEM((TILES, BLK, BLK), jnp.int32),
        pltpu.VMEM((2, 4, 4, BLK, CH), BF),
        pltpu.VMEM((2, 4, 4, BLK, CH), BF),
        pltpu.VMEM((4, 4, BLK, CH), BF),
        pltpu.VMEM((4, 4, BLK, CH), BF),
        pltpu.VMEM((4 * CH, CH), BF),
        pltpu.VMEM((4 * CH, CH), BF),
        pltpu.VMEM((NODES, CH), BF),
        pltpu.VMEM((2 * SLOTS + T2, 2, BLK, BLK), BF),
        pltpu.VMEM((SLOTS, 2, BLK, BLK), BF),
        pltpu.VMEM((2 * SLOTS, 2, BLK, BLK), BF),
        pltpu.VMEM((SLOTS, 2, BLK, BLK), BF),
        pltpu.VMEM((T2, 2, BLK, BLK), BF),
        pltpu.VMEM((2, NODES, SLOTS * BLK), BF),
        pltpu.VMEM((2, SLOTS * BLK, CH), BF),
        pltpu.VMEM((2, NODES, CH), F32),
        pltpu.VMEM((3, 2, NODES, CH), BF),
        pltpu.VMEM((3, 2, NODES, CH), BF),
        pltpu.VMEM((4, 2, NODES, CH), BF),
        pltpu.VMEM((4, 2, 4, 32, 4 * CH), F32),
        pltpu.VMEM((4, 4, 32, 4 * CH), F32),
        pltpu.VMEM((4, 4, 32, 4 * CH), F32),
        pltpu.VMEM((4, 4, 32, 4 * CH), BF),
        pltpu.VMEM((4, 3, 32, 4 * CH), BF),
        pltpu.VMEM((3, 32, 4 * CH), BF),
        pltpu.VMEM((3, 32, 4 * CH), BF),
        pltpu.VMEM((2, 4, 16, CH), F32),
        pltpu.VMEM((7, 16, CH), F32),
        dma((8,)),
        dma((2,)),
        dma((2,)),
        dma((4,)),
        dma((4,)),
        dma((4,)),
        dma((4,)),
        dma((4,)),
        dma((4,)),
        dma,
        dma,
        dma((6,)),
        dma((6,)),
        dma((4,)),
        dma((4,)),
        dma((4, 3)),
        dma((4, 3)),
        dma((3,)),
        dma((3,)),
        dma((7,)),
        dma((7,)),
        dma((3,)),
        dma((3,)),
        dma((3,)),
        dma((3,)),
    ]
    hidden_nodes, node_grad, w_dec_grad = pl.pallas_call(
        kernel,
        out_shape=(
            jax.ShapeDtypeStruct((NODES, CH), BF),
            jax.ShapeDtypeStruct((NODES, CH), BF),
            jax.ShapeDtypeStruct((16, CH), F32),
        ),
        in_specs=[pl.BlockSpec(memory_space=pltpu.SMEM)] + [hbm] * 7,
        out_specs=(vmem, vmem, vmem),
        scratch_shapes=scratch,
        compiler_params=pltpu.CompilerParams(
            collective_id=0, has_side_effects=True, vmem_limit_bytes=60 * 1024 * 1024
        ),
        name="encode_and_backward",
    )(
        table,
        cells_next.reshape(4, 4, BLK, CH),
        node_embed,
        enc_mix,
        out_cotangent.reshape(4, 4, BLK, CH),
        decoded_saved.reshape(4, 4, BLK, CH),
        dec_proj,
        tile_codes.reshape(TILES, BLK, BLK),
    )
    return hidden_nodes, node_grad, w_dec_grad


def solution(mesh):
    in_specs = (
        P("band", "chan"),
        P("band", "chan"),
        P(None, "chan"),
        P("band", "chan"),
        P("band", "chan"),
        P(None, "chan"),
        P(),
        P("band", None, None, None),
    )
    out_specs = (P("band", "chan"), P("band", "chan"), P("band", "chan"))
    return jax.shard_map(shards, mesh=mesh, in_specs=in_specs, out_specs=out_specs, check_vma=False)
```

time: 333 us -> 249 us (0.75)
  the two profiles are of different devices: /device:TPU:32 before, /device:TPU:8 now
where the time goes in v1:
time: 249 us; the launch traced here: 248 us
  Pallas kernels  240 us (96%)
  local copies, waits for them, and re-layouts  6.08 us (2%)
    pallas_call x1, Pallas kernels, shards(): pl.pallas_call(kernel, out_shape=(jax.ShapeDtypeStruct((NODES, CH), BF),...  240 us
    unnamed x4, local copies, waits for them, and re-layouts  5.26 us

profile of v1, /device:TPU:8, one launch (start us, length us, event | category | flops | bytes accessed | tf_op | source)
XLA Modules:
  0.0 248.3 jit_solution(9803922979813549549)
XLA Ops:
  0.7 0.1 stack.42
  0.8 0.1 stack.47
  1.0 0.8 copy.13
  1.8 0.1 reshape.511
  1.8 0.6 gather_fusion
  2.4 0.1 fusion.1
  2.5 0.1 fusion.3
  2.5 0.2 convert_reduce_fusion
  2.8 0.8 select_reduce_fusion.table
  3.6 240.2 %encode_and_backward.1 = (bf16[256,256]{1,0:T(8,128)(2,1)}, bf16[256,256]{1,0:T(8,128)(2,1)}, f32[16,256]{1,0:T(8,128)}) custom-call(s32[8,16]{1,0:T(8,128)} %select_reduce_fusion.table, bf16[4,4,128,256]{3,2,1,0:T(8,128)(2,1)} %bitcast.15, bf16[256,256]{1,0:T(8,128)(2,1)} %embed_hbm.1, bf16[1024,256]{1,0:T(8,128)(2,1)} %mix_hbm.1, ...), custom_call_target="tpu_custom_call" | custom-call | tf_op jit(solution)/shard_map/encode_and_backward/pallas_call | solution.py:533
  243.8 1.6 copy.17
  245.4 1.6 copy.18
  246.9 1.3 copy.19
  (5 shorter events, 0.0 us)

commit v2 on v1

--- a/solution.py
+++ b/solution.py
@@ -21,9 +21,9 @@
 BF = jnp.bfloat16
 F32 = jnp.float32
 
-UP = (0, 4, 16, 20)
-DOWN = (8, 12, 24, 28)
-CHUNK = 4
+CHUNK = 2
+STEPS = 8
+A_TICKS = (1, 3, 5, 7, 8, 9)
 
 
 def chip_links(chip, z_hi, core):
@@ -196,16 +196,21 @@
     z_up = at_chip(jnp.where(q == 3, across, chip), (q + 1) % 4)
     z_down = at_chip(jnp.where(q == 0, across, chip), (q + 3) % 4)
 
+    def up_part(step):
+        return pl.ds(CHUNK * step + 8 * (step // 4), CHUNK)
+
+    def down_part(step):
+        return pl.ds(CHUNK * step + 8 * (step // 4) + 8, CHUNK)
+
     def up_copy(step, src):
-        part = pl.ds(UP[step], CHUNK)
+        part = up_part(step)
         return remote(src.at[part], got_z.at[part], up_send.at[step], up_recv.at[step], z_up)
 
     def down_copy(step, src):
-        part = pl.ds(DOWN[step], CHUNK)
+        part = down_part(step)
         return remote(src.at[part], got_z.at[part], down_send.at[step], down_recv.at[step], z_down)
 
-    def relay_copy(index, start):
-        part = pl.ds(start, CHUNK)
+    def relay_copy(index, part):
         return remote(
             got_z.at[part],
             got_y.at[part],
@@ -214,11 +219,7 @@
             at_chip(relay_to, q),
         )
 
-    relays = [
-        relay_copy(index, start)
-        for index, start in enumerate((UP[0], DOWN[0], UP[1], DOWN[1]))
-    ]
-    for step in range(4):
+    for step in range(STEPS):
 
         @pl.when(q == 3)
         def _(step=step):
@@ -247,23 +248,34 @@
             )
     waiting = list(a_copies)
 
-    for step in range(4):
-        up_copy(step, got_z).wait_recv()
-
-        @pl.when(q < 3)
-        def _(step=step):
-            up_copy(step, got_z).start()
-
-        down_copy(step, got_z).wait_recv()
-
-        @pl.when(q > 0)
-        def _(step=step):
-            down_copy(step, got_z).start()
-
-        if step < 2:
-            relays[2 * step].start()
-            relays[2 * step + 1].start()
-        for _ in range(1 if step < 2 else 2):
+    for tick in range(STEPS + 3):
+        up, down = tick - q, tick - 3 + q
+
+        @pl.when((up >= 0) & (up < STEPS))
+        def _(step=up):
+            up_copy(step, got_z).wait_recv()
+
+            @pl.when(q < 3)
+            def _():
+                up_copy(step, got_z).start()
+
+            @pl.when(step < 4)
+            def _():
+                relay_copy(step, up_part(step)).start()
+
+        @pl.when((down >= 0) & (down < STEPS))
+        def _(step=down):
+            down_copy(step, got_z).wait_recv()
+
+            @pl.when(q > 0)
+            def _():
+                down_copy(step, got_z).start()
+
+            @pl.when(step < 4)
+            def _():
+                relay_copy(step + 4, down_part(step)).start()
+
+        if tick in A_TICKS:
             waiting.pop(0).start()
 
     def sums(row, count, tiles, base):
@@ -314,8 +326,9 @@
     send_part(0, 5, SLOTS, got_z, 16)
     two.wait_recv()
     send_part(1, 6, T2, got_two, 0)
-    for copy in relays:
-        copy.wait_recv()
+    for step in range(4):
+        relay_copy(step, up_part(step)).wait_recv()
+        relay_copy(step + 4, down_part(step)).wait_recv()
     send_part(2, 4, SLOTS, got_y, 0)
     pack(3, SLOTS, own_packed, 0)
     result = sums(7, SLOTS, own_packed, 0)
@@ -458,11 +471,12 @@
         total = total + z_recv[index]
     w_out[...] = total * (ROWS * 64) ** (-0.5)
 
-    for step in range(4):
+    for step in range(STEPS):
         up_copy(step, got_z).wait_send()
         down_copy(step, got_z).wait_send()
+        relay_copy(step, up_part(step % 4)).wait_send()
     two.wait_send()
-    ends = relays + shares + a_copies + part_copies + core_copies + agg_copies + z_copies
+    ends = shares + a_copies + part_copies + core_copies + agg_copies + z_copies
     for copy in ends + list(y_copies.values()) + list(x_copies.values()):
         copy.wait_send()
 
@@ -507,12 +521,12 @@
         dma((8,)),
         dma((2,)),
         dma((2,)),
-        dma((4,)),
-        dma((4,)),
-        dma((4,)),
-        dma((4,)),
-        dma((4,)),
-        dma((4,)),
+        dma((8,)),
+        dma((8,)),
+        dma((8,)),
+        dma((8,)),
+        dma((8,)),
+        dma((8,)),
         dma,
         dma,
         dma((6,)),

time: 249 us -> 156 us (0.63)
  the two profiles are of different devices: /device:TPU:8 before, /device:TPU:32 now
where the time goes in v2:
time: 156 us; the launch traced here: 155 us
  Pallas kernels  147 us (94%)
  local copies, waits for them, and re-layouts  6.08 us (4%)
    pallas_call x1, Pallas kernels, shards(): pl.pallas_call(kernel, out_shape=(jax.ShapeDtypeStruct((NODES, CH), BF),...  147 us
    unnamed x4, local copies, waits for them, and re-layouts  5.26 us

profile of v2, /device:TPU:32, one launch (start us, length us, event | category | flops | bytes accessed | tf_op | source)
XLA Modules:
  0.0 155.4 jit_solution(17550242135229881615)
XLA Ops:
  0.7 0.1 stack.42
  0.8 0.1 stack.47
  1.0 0.8 copy.13
  1.8 0.1 reshape.511
  1.8 0.6 gather_fusion
  2.4 0.1 fusion.1
  2.5 0.1 fusion.3
  2.5 0.2 convert_reduce_fusion
  2.8 0.8 select_reduce_fusion.table
  3.6 147.4 %encode_and_backward.1 = (bf16[256,256]{1,0:T(8,128)(2,1)}, bf16[256,256]{1,0:T(8,128)(2,1)}, f32[16,256]{1,0:T(8,128)}) custom-call(s32[8,16]{1,0:T(8,128)} %select_reduce_fusion.table, bf16[4,4,128,256]{3,2,1,0:T(8,128)(2,1)} %bitcast.15, bf16[256,256]{1,0:T(8,128)(2,1)} %embed_hbm.1, bf16[1024,256]{1,0:T(8,128)(2,1)} %mix_hbm.1, ...), custom_call_target="tpu_custom_call" | custom-call | tf_op jit(solution)/shard_map/encode_and_backward/pallas_call | solution.py:547
  151.0 1.6 %copy.17 = bf16[256,256]{1,0:T(8,128)(2,1)} copy(bf16[256,256]{1,0:T(8,128)(2,1)} %get-tuple-element.8) | data formatting | bytes 262144
  152.5 1.6 %copy.18 = bf16[256,256]{1,0:T(8,128)(2,1)} copy(bf16[256,256]{1,0:T(8,128)(2,1)} %get-tuple-element.9) | data formatting | bytes 262144
  154.1 1.3 copy.19
  (5 shorter events, 0.0 us)

commit v3 on v2

--- a/solution.py
+++ b/solution.py
@@ -22,8 +22,13 @@
 F32 = jnp.float32
 
 CHUNK = 2
-STEPS = 8
-A_TICKS = (1, 3, 5, 7, 8, 9)
+STEPS = 10
+SHORT = 6
+A_FIRST = 4
+A_TICKS = (1,1,1,1,1,1,1,1,0,0,0)
+TWO_TICK = 5
+OWN_TICK = 6
+BEYOND_TICK = 8
 
 
 def chip_links(chip, z_hi, core):
@@ -83,6 +88,9 @@
     lhs,
     rhs,
     own_sum,
+    side_sum,
+    beyond_send,
+    beyond_recv,
     part_send,
     part_recv,
     agg_all,
@@ -116,10 +124,13 @@
     x_recv_sem,
     z_send_sem,
     z_recv_sem,
+    beyond_send_sem,
+    beyond_recv_sem,
     part_send_sem,
     part_recv_sem,
     agg_send_sem,
     agg_recv_sem,
+    hop_send_sem,
 ):
     band = lax.axis_index("band")
     q = lax.axis_index("chan")
@@ -156,7 +167,7 @@
         + along_q
         + along_y
         + along_x
-        + [at_chip(two_to, q), at_chip(two_from, q), at_chip(beyond, q)]
+        + [at_chip(two_to, q), at_chip(two_from, q)]
     )
     for partner in partners:
         pl.semaphore_signal(barrier, inc=1, device_id=partner, device_id_type=MESH)
@@ -187,20 +198,40 @@
 
         lax.fori_loop(0, count, one, 0)
 
+    a_copies = []
+    for half in range(2):
+        for d in (1, 3, 2):
+            other = (q + d) % 4
+            for array, (src, dst) in enumerate(((cot_hbm, cot_all), (saved_hbm, saved_all))):
+                index = 2 * (d - 1) + array
+                part = pl.ds(2 * half, 2)
+                a_copies.append(
+                    remote(
+                        src.at[other, part],
+                        dst.at[q, part],
+                        a_send.at[half, index],
+                        a_recv.at[half, index],
+                        (band, other),
+                    )
+                )
+    waiting = list(a_copies)
+
+    pl.semaphore_wait(barrier, len(partners))
+    for _ in range(A_FIRST):
+        waiting.pop(0).start()
     loads[0].wait()
     pack(0, SLOTS, packed, 0)
     pack(1, SLOTS, packed, 16)
     pack(2, T2, packed, 32)
-    pl.semaphore_wait(barrier, len(partners))
 
     z_up = at_chip(jnp.where(q == 3, across, chip), (q + 1) % 4)
     z_down = at_chip(jnp.where(q == 0, across, chip), (q + 3) % 4)
 
     def up_part(step):
-        return pl.ds(CHUNK * step + 8 * (step // 4), CHUNK)
+        return pl.ds(CHUNK * step + 8 * (step // 4) - 4 * (step // 8), CHUNK)
 
     def down_part(step):
-        return pl.ds(CHUNK * step + 8 * (step // 4) + 8, CHUNK)
+        return pl.ds(CHUNK * step + 8 + 8 * (step // 4) - 20 * (step // 8), CHUNK)
 
     def up_copy(step, src):
         part = up_part(step)
@@ -237,46 +268,6 @@
     ]
     for share in shares:
         share.start()
-
-    a_copies = []
-    for d in range(1, 4):
-        other = (q + d) % 4
-        for array, (src, dst) in enumerate(((cot_hbm, cot_all), (saved_hbm, saved_all))):
-            index = 2 * (d - 1) + array
-            a_copies.append(
-                remote(src.at[other], dst.at[q], a_send.at[index], a_recv.at[index], (band, other))
-            )
-    waiting = list(a_copies)
-
-    for tick in range(STEPS + 3):
-        up, down = tick - q, tick - 3 + q
-
-        @pl.when((up >= 0) & (up < STEPS))
-        def _(step=up):
-            up_copy(step, got_z).wait_recv()
-
-            @pl.when(q < 3)
-            def _():
-                up_copy(step, got_z).start()
-
-            @pl.when(step < 4)
-            def _():
-                relay_copy(step, up_part(step)).start()
-
-        @pl.when((down >= 0) & (down < STEPS))
-        def _(step=down):
-            down_copy(step, got_z).wait_recv()
-
-            @pl.when(q > 0)
-            def _():
-                down_copy(step, got_z).start()
-
-            @pl.when(step < 4)
-            def _():
-                relay_copy(step + 4, down_part(step)).start()
-
-        if tick in A_TICKS:
-            waiting.pop(0).start()
 
     def sums(row, count, tiles, base):
         def one(s, carry):
@@ -304,36 +295,103 @@
             for which in range(2)
         ]
 
-    for load in loads[1:3]:
-        load.wait()
-    for share in shares:
-        share.wait_recv()
-
-    part_to = [at_chip(across, q), at_chip(two_from, q), at_chip(beyond, q)]
+    beyond_copies = [
+        remote(
+            beyond_send.at[which],
+            beyond_recv.at[which],
+            beyond_send_sem.at[which],
+            beyond_recv_sem.at[which],
+            at_chip((chip - 2 * (1 - 2 * h) + CHIPS) % CHIPS, q),
+        )
+        for which in range(2)
+    ]
+
+    def send_beyond():
+        for step in range(4):
+            relay_copy(step, up_part(step)).wait_recv()
+            relay_copy(step + 4, down_part(step)).wait_recv()
+        result = sums(4, SLOTS, got_y, 0)
+        for which in range(2):
+            beyond_send[which] = result[which].astype(BF)
+            beyond_copies[which].start()
+
     part_copies = [
-        remote(
-            part_send.at[g], part_recv.at[g], part_send_sem.at[g], part_recv_sem.at[g], part_to[g]
-        )
-        for g in range(3)
+        [
+            remote(
+                part_send.at[g, which],
+                part_recv.at[g, which],
+                part_send_sem.at[g, which],
+                part_recv_sem.at[g, which],
+                at_chip(to, q),
+            )
+            for which in range(2)
+        ]
+        for g, to in enumerate((across, two_from))
     ]
 
-    def send_part(g, row, count, tiles, base):
-        result = sums(row, count, tiles, base)
+    def send_two():
+        two.wait_recv()
+        result = sums(6, T2, got_two, 0)
         for which in range(2):
-            part_send[g, which] = result[which].astype(BF)
-        part_copies[g].start()
-
-    send_part(0, 5, SLOTS, got_z, 16)
-    two.wait_recv()
-    send_part(1, 6, T2, got_two, 0)
-    for step in range(4):
-        relay_copy(step, up_part(step)).wait_recv()
-        relay_copy(step + 4, down_part(step)).wait_recv()
-    send_part(2, 4, SLOTS, got_y, 0)
-    pack(3, SLOTS, own_packed, 0)
-    result = sums(7, SLOTS, own_packed, 0)
+            part_send[1, which] = result[which].astype(BF)
+            part_copies[1][which].start()
+
+    def sum_own():
+        pack(3, SLOTS, own_packed, 0)
+        result = sums(7, SLOTS, own_packed, 0)
+        for which in range(2):
+            own_sum[which] = result[which]
+
+    for tick in range(STEPS + 1):
+        if tick == TWO_TICK:
+            for load in loads[1:3]:
+                load.wait()
+            for share in shares:
+                share.wait_recv()
+            send_two()
+        if tick == OWN_TICK:
+            sum_own()
+        if tick == BEYOND_TICK:
+            send_beyond()
+        up, down = tick - q, tick - 3 + q
+
+        @pl.when((up >= 0) & (up < STEPS) & ((up < SHORT) | (q < 2)))
+        def _(step=up):
+            up_copy(step, got_z).wait_recv()
+
+            @pl.when((q < 3) & ((step < SHORT) | (q < 1)))
+            def _():
+                up_copy(step, got_z).start()
+
+            @pl.when(step < 4)
+            def _():
+                relay_copy(step, up_part(step)).start()
+
+        @pl.when((down >= 0) & (down < STEPS) & ((down < SHORT) | (q > 1)))
+        def _(step=down):
+            down_copy(step, got_z).wait_recv()
+
+            @pl.when((q > 0) & ((step < SHORT) | (q > 2)))
+            def _():
+                down_copy(step, got_z).start()
+
+            @pl.when(step < 4)
+            def _():
+                relay_copy(step + 4, down_part(step)).start()
+
+        for _ in range(A_TICKS[tick]):
+            waiting.pop(0).start()
+
+    result = sums(5, SLOTS, got_z, 16)
     for which in range(2):
-        own_sum[which] = result[which]
+        side_sum[which] = result[which]
+    for which in range(2):
+        beyond_copies[which].wait_recv()
+        total = side_sum[which] + beyond_recv[which].astype(F32)
+        part_send[0, which] = total.astype(BF)
+        part_copies[0][which].start()
+    for copy in waiting:
+        copy.start()
 
     for load in loads[3:5]:
         load.wait()
@@ -390,21 +448,41 @@
             )
             y_copies[d, e].start()
 
-    for copy in part_copies:
-        copy.wait_recv()
+    def agg_copy(d, which):
+        return remote(
+            agg_all.at[q, which],
+            agg_all.at[q, which],
+            agg_send_sem.at[d - 1, which],
+            agg_recv_sem.at[d - 1, which],
+            (band, (q + d) % 4),
+        )
+
+    def hop_copy(which):
+        block = (q + 2) % 4
+        return remote(
+            agg_all.at[block, which],
+            agg_all.at[block, which],
+            hop_send_sem.at[which],
+            agg_recv_sem.at[2 * (q - 1), which],
+            (band, 3 * (q - 1)),
+        )
+
+    middle = (q == 1) | (q == 2)
+
+    def far(d):
+        return ((q == 0) & (d == 3)) | ((q == 3) & (d == 1))
+
     for which in range(2):
         total = own_sum[which]
-        for g in range(3):
+        for g in range(2):
+            part_copies[g][which].wait_recv()
             total = total + part_recv[g, which].astype(F32)
         agg_all[q, which] = (total * SCALE).astype(BF)
-    agg_copies = [
-        remote(
-            agg_all.at[q], agg_all.at[q], agg_send_sem.at[d], agg_recv_sem.at[d], along_q[d]
-        )
-        for d in range(3)
-    ]
-    for copy in agg_copies:
-        copy.start()
+        for d in (2, 1, 3):
+
+            @pl.when(jnp.logical_not(far(d)))
+            def _(d=d, which=which):
+                agg_copy(d, which).start()
 
     x_copies = {}
     for d in order:
@@ -422,6 +500,13 @@
                 along_x[d - 1],
             )
             x_copies[d].start()
+    for which in range(2):
+        agg_copy(2, which).wait_recv()
+
+        @pl.when(middle)
+        def _(which=which):
+            hop_copy(which).start()
+
     for d in range(1, 4):
         x_copies[d].wait_recv()
         total = total + x_recv[d - 1].astype(F32)
@@ -450,8 +535,8 @@
 
     for load in loads[5:8]:
         load.wait()
-    for copy in agg_copies:
-        copy.wait_recv()
+    for d in (1, 3):
+        agg_copy(d, 0).wait_recv()
     mixed = jnp.zeros((NODES, CH), F32)
     grad = jnp.zeros((NODES, CH), F32)
     for j in range(4):
@@ -459,6 +544,8 @@
             agg_all[j, 0], mix[pl.ds(j * CH, CH), :], preferred_element_type=F32
         )
     hidden_out[...] = (embed[...].astype(F32) + mixed / (1.0 + jnp.exp(-mixed))).astype(BF)
+    for d in (1, 3):
+        agg_copy(d, 1).wait_recv()
     for j in range(4):
         grad = grad + jnp.dot(
             agg_all[j, 1], proj[pl.ds(j * CH, CH), :], preferred_element_type=F32
@@ -472,11 +559,29 @@
     w_out[...] = total * (ROWS * 64) ** (-0.5)
 
     for step in range(STEPS):
-        up_copy(step, got_z).wait_send()
-        down_copy(step, got_z).wait_send()
-        relay_copy(step, up_part(step % 4)).wait_send()
+
+        @pl.when((q == 0) | (q == 3) | (step < SHORT))
+        def _(step=step):
+            up_copy(step, got_z).wait_send()
+            down_copy(step, got_z).wait_send()
+
+    for step in range(4):
+        relay_copy(step, up_part(step)).wait_send()
+        relay_copy(step + 4, down_part(step)).wait_send()
     two.wait_send()
-    ends = shares + a_copies + part_copies + core_copies + agg_copies + z_copies
+    for which in range(2):
+        for d in range(1, 4):
+
+            @pl.when(jnp.logical_not(far(d)))
+            def _(d=d, which=which):
+                agg_copy(d, which).wait_send()
+
+        @pl.when(middle)
+        def _(which=which):
+            hop_copy(which).wait_send()
+
+    ends = shares + a_copies + beyond_copies + part_copies[0] + part_copies[1]
+    ends = ends + core_copies + z_copies
     for copy in ends + list(y_copies.values()) + list(x_copies.values()):
         copy.wait_send()
 
@@ -506,8 +611,11 @@
         pltpu.VMEM((2, NODES, SLOTS * BLK), BF),
         pltpu.VMEM((2, SLOTS * BLK, CH), BF),
         pltpu.VMEM((2, NODES, CH), F32),
-        pltpu.VMEM((3, 2, NODES, CH), BF),
-        pltpu.VMEM((3, 2, NODES, CH), BF),
+        pltpu.VMEM((2, NODES, CH), F32),
+        pltpu.VMEM((2, NODES, CH), BF),
+        pltpu.VMEM((2, NODES, CH), BF),
+        pltpu.VMEM((2, 2, NODES, CH), BF),
+        pltpu.VMEM((2, 2, NODES, CH), BF),
         pltpu.VMEM((4, 2, NODES, CH), BF),
         pltpu.VMEM((4, 2, 4, 32, 4 * CH), F32),
         pltpu.VMEM((4, 4, 32, 4 * CH), F32),
@@ -521,16 +629,16 @@
         dma((8,)),
         dma((2,)),
         dma((2,)),
-        dma((8,)),
-        dma((8,)),
-        dma((8,)),
-        dma((8,)),
+        dma((10,)),
+        dma((10,)),
+        dma((10,)),
+        dma((10,)),
         dma((8,)),
         dma((8,)),
         dma,
         dma,
-        dma((6,)),
-        dma((6,)),
+        dma((2, 6)),
+        dma((2, 6)),
         dma((4,)),
         dma((4,)),
         dma((4, 3)),
@@ -539,10 +647,13 @@
         dma((3,)),
         dma((7,)),
         dma((7,)),
-        dma((3,)),
-        dma((3,)),
-        dma((3,)),
-        dma((3,)),
+        dma((2,)),
+        dma((2,)),
+        dma((2, 2)),
+        dma((2, 2)),
+        dma((3, 2)),
+        dma((3, 2)),
+        dma((2,)),
     ]
     hidden_nodes, node_grad, w_dec_grad = pl.pallas_call(
         kernel,

time: 156 us -> 126 us (0.81)
  Pallas kernels: 147 us -> 116 us
    pallas_call x1, Pallas kernels: 147 us -> 116 us  [shards(): pl.pallas_call(kernel, out_shape=(jax.ShapeDtypeStruct((NODES, CH), BF),...]
where the time goes in v3:
time: 126 us; the launch traced here: 124 us
  Pallas kernels  116 us (92%)
  local copies, waits for them, and re-layouts  6.08 us (5%)
    pallas_call x1, Pallas kernels, shards(): pl.pallas_call(kernel, out_shape=(jax.ShapeDtypeStruct((NODES, CH), BF),...  116 us
    unnamed x4, local copies, waits for them, and re-layouts  5.26 us

profile of v3, /device:TPU:32, one launch (start us, length us, event | category | flops | bytes accessed | tf_op | source)
XLA Modules:
  0.0 124.3 jit_solution(12513194778250836068)
XLA Ops:
  0.7 0.1 stack.42
  0.8 0.1 stack.47
  1.0 0.8 copy.13
  1.8 0.1 reshape.511
  1.8 0.6 gather_fusion
  2.4 0.1 fusion.1
  2.5 0.1 fusion.3
  2.5 0.2 convert_reduce_fusion
  2.8 0.8 select_reduce_fusion.table
  3.6 116.2 %encode_and_backward.1 = (bf16[256,256]{1,0:T(8,128)(2,1)}, bf16[256,256]{1,0:T(8,128)(2,1)}, f32[16,256]{1,0:T(8,128)}) custom-call(s32[8,16]{1,0:T(8,128)} %select_reduce_fusion.table, bf16[4,4,128,256]{3,2,1,0:T(8,128)(2,1)} %bitcast.15, bf16[256,256]{1,0:T(8,128)(2,1)} %embed_hbm.1, bf16[1024,256]{1,0:T(8,128)(2,1)} %mix_hbm.1, ...), custom_call_target="tpu_custom_call" | custom-call | tf_op jit(solution)/shard_map/encode_and_backward/pallas_call | solution.py:658
  119.8 1.6 %copy.17 = bf16[256,256]{1,0:T(8,128)(2,1)} copy(bf16[256,256]{1,0:T(8,128)(2,1)} %get-tuple-element.8) | data formatting | bytes 262144
  121.4 1.6 %copy.18 = bf16[256,256]{1,0:T(8,128)(2,1)} copy(bf16[256,256]{1,0:T(8,128)(2,1)} %get-tuple-element.9) | data formatting | bytes 262144
  122.9 1.3 %copy.19 = f32[16,256]{1,0:T(8,128)} copy(f32[16,256]{1,0:T(8,128)} %get-tuple-element.10) | data formatting | bytes 32768
  (5 shorter events, 0.0 us)

commit v4 on v3

--- a/solution.py
+++ b/solution.py
@@ -21,14 +21,15 @@
 BF = jnp.bfloat16
 F32 = jnp.float32
 
+Z_SLOTS = 24
 CHUNK = 2
-STEPS = 10
-SHORT = 6
+STEPS = 8
+SHORT = 4
 A_FIRST = 4
-A_TICKS = (1,1,1,1,1,1,1,1,0,0,0)
-TWO_TICK = 5
-OWN_TICK = 6
-BEYOND_TICK = 8
+A_TICKS = (1, 1, 1, 1, 1, 1, 1, 1, 0)
+TWO_TICK = 4
+OWN_TICK = 5
+BEYOND_TICK = 7
 
 
 def chip_links(chip, z_hi, core):
@@ -41,27 +42,8 @@
     return across, beyond, relay_to, two_to, two_from
 
 
-def slot_tables(tile_source, my_band):
-    chip, core = my_band // 2, my_band % 2
-    across, beyond, _, two_to, two_from = chip_links(chip, chip % 2, core)
-    targets = jnp.stack(
-        [my_band] * 4 + [2 * beyond + core, 2 * across + core, 2 * two_from + core, my_band]
-    )
-    sources = jnp.stack([beyond, across, two_to, chip, chip, chip, chip, chip])
-    blocks = tile_source.reshape(-1, TILES)[targets]
-    tile = jnp.arange(TILES, dtype=jnp.int32)
-    match = (blocks // 32) == sources[:, None]
-    before = tile[None, :, None] > tile[None, None, :]
-    rank = jnp.sum((match[:, None, :] & before).astype(jnp.int32), axis=2)
-    sending = (jnp.arange(8) < 4)[:, None]
-    entry = jnp.where(sending, tile[None, :] + 256, blocks % 32 + 256 * (tile[None, :] // K))
-    slot = jnp.arange(SLOTS, dtype=jnp.int32)
-    chosen = match[:, :, None] & (rank[:, :, None] == slot[None, None, :])
-    return jnp.sum(jnp.where(chosen, entry[:, :, None], 0), axis=1)
-
-
 def kernel(
-    table,
+    source,
     cells_hbm,
     embed_hbm,
     mix_hbm,
@@ -72,6 +54,8 @@
     hidden_out,
     grad_out,
     w_out,
+    table,
+    table_rows,
     codes,
     cells,
     cot,
@@ -185,6 +169,47 @@
     for load in loads:
         load.start()
 
+    lane = lax.broadcasted_iota(jnp.int32, (8, BLK), 1)
+    row = lax.broadcasted_iota(jnp.int32, (8, BLK), 0)
+
+    def place(t, carry):
+        rows, ranks = carry
+        own, far, near, two = (
+            source[t % K, 2 * owner + t // K]
+            for owner in (band, 2 * beyond + core, 2 * across + core, 2 * two_from + core)
+        )
+        hits = (
+            own // 32 == beyond,
+            own // 32 == across,
+            own // 32 == two_to,
+            own // 32 == chip,
+            far // 32 == chip,
+            near // 32 == chip,
+            two // 32 == chip,
+        )
+        half = 256 * (t // K) + 512
+        entries = (
+            (0, hits[0], ranks[0], t + 256),
+            (0, hits[1], Z_SLOTS - 1 - ranks[1], t + 256),
+            (2, hits[2], ranks[2], t + 256),
+            (3, hits[3], ranks[3], t + 256),
+            (4, hits[4], ranks[4], far % 32 + half + 1024 * ranks[4]),
+            (5, hits[5], ranks[5], near % 32 + half + 1024 * (Z_SLOTS - 1 - ranks[5])),
+            (6, hits[6], ranks[6], two % 32 + half + 1024 * ranks[6]),
+            (7, hits[3], ranks[3], own % 32 + half + 1024 * ranks[3]),
+        )
+        for index, hit, slot, value in entries:
+            spot = (row == index) & (lane == jnp.where(hit, slot, -1))
+            rows = jnp.where(spot, value, rows)
+        ranks = tuple(rank + jnp.where(hit, 1, 0) for rank, hit in zip(ranks, hits))
+        return rows, ranks
+
+    zero = jnp.int32(0)
+    table_rows[...] = lax.fori_loop(
+        0, TILES, place, (jnp.zeros((8, BLK), jnp.int32), (zero,) * 7)
+    )[0]
+    table_load = pltpu.make_async_copy(table_rows, table, load_sem.at[8])
+
     def pack(row, count, dest, base):
         def one(s, carry):
             item = table[row, s]
@@ -219,19 +244,20 @@
     pl.semaphore_wait(barrier, len(partners))
     for _ in range(A_FIRST):
         waiting.pop(0).start()
+    table_load.start()
     loads[0].wait()
-    pack(0, SLOTS, packed, 0)
-    pack(1, SLOTS, packed, 16)
-    pack(2, T2, packed, 32)
+    table_load.wait()
+    pack(0, Z_SLOTS, packed, 0)
+    pack(2, T2, packed, Z_SLOTS)
 
     z_up = at_chip(jnp.where(q == 3, across, chip), (q + 1) % 4)
     z_down = at_chip(jnp.where(q == 0, across, chip), (q + 3) % 4)
 
     def up_part(step):
-        return pl.ds(CHUNK * step + 8 * (step // 4) - 4 * (step // 8), CHUNK)
+        return pl.ds(CHUNK * step + 8 * (step // SHORT), CHUNK)
 
     def down_part(step):
-        return pl.ds(CHUNK * step + 8 + 8 * (step // 4) - 20 * (step // 8), CHUNK)
+        return pl.ds(CHUNK * step + 8, CHUNK)
 
     def up_copy(step, src):
         part = up_part(step)
@@ -260,7 +286,7 @@
         def _(step=step):
             down_copy(step, packed).start()
 
-    two = remote(packed.at[pl.ds(32, T2)], got_two, two_send, two_recv, at_chip(two_to, q))
+    two = remote(packed.at[pl.ds(Z_SLOTS, T2)], got_two, two_send, two_recv, at_chip(two_to, q))
     two.start()
     shares = [
         remote(cells_hbm, cells.at[core], share_send.at[0], share_recv.at[0], sibling),
@@ -269,14 +295,14 @@
     for share in shares:
         share.start()
 
-    def sums(row, count, tiles, base):
+    def sums(row, count, tiles):
         def one(s, carry):
             item = table[row, s]
             column = pl.ds(pl.multiple_of(s * BLK, BLK), BLK)
-            first = jnp.where(item < 256, 1.0, 0.0).astype(BF)
-            second = jnp.where(item < 256, 0.0, 1.0).astype(BF)
+            first = jnp.where((item & 768) == 512, 1.0, 0.0).astype(BF)
+            second = jnp.where((item & 768) == 768, 1.0, 0.0).astype(BF)
             for which in range(2):
-                tile = tiles[base + s, which]
+                tile = tiles[item // 1024, which]
                 lhs[which, pl.ds(0, BLK), column] = tile * first
                 lhs[which, pl.ds(BLK, BLK), column] = tile * second
             block = item & 31
@@ -310,7 +336,7 @@
         for step in range(4):
             relay_copy(step, up_part(step)).wait_recv()
             relay_copy(step + 4, down_part(step)).wait_recv()
-        result = sums(4, SLOTS, got_y, 0)
+        result = sums(4, SLOTS, got_y)
         for which in range(2):
             beyond_send[which] = result[which].astype(BF)
             beyond_copies[which].start()
@@ -331,16 +357,56 @@
 
     def send_two():
         two.wait_recv()
-        result = sums(6, T2, got_two, 0)
+        result = sums(6, T2, got_two)
         for which in range(2):
             part_send[1, which] = result[which].astype(BF)
             part_copies[1][which].start()
 
     def sum_own():
         pack(3, SLOTS, own_packed, 0)
-        result = sums(7, SLOTS, own_packed, 0)
+        result = sums(7, SLOTS, own_packed)
         for which in range(2):
             own_sum[which] = result[which]
+
+    core_copies = [
+        remote(
+            w_part.at[d, 1 - core],
+            core_recv.at[d],
+            core_send_sem.at[d],
+            core_recv_sem.at[d],
+            sibling,
+        )
+        for d in range(4)
+    ]
+    order = (1, 2, 3, 0)
+
+    def start_projection():
+        for load in loads[3:5]:
+            load.wait()
+        for copy in a_copies:
+            copy.wait_recv()
+
+        for d in order:
+            left = cot_all.at[(x + d) % 4]
+
+            def columns(j, carry, d=d, left=left):
+                product = lax.dot_general(
+                    left[...].reshape(QROWS, CH),
+                    saved_all[j].reshape(QROWS, CH),
+                    (((0,), (0,)), ((), ())),
+                    preferred_element_type=F32,
+                )
+                span = pl.ds(pl.multiple_of(j * CH, CH), CH)
+                for group in range(8):
+                    for half in range(2):
+                        start = (2 * group + half) * 16
+                        w_part[d, half, group // 2, pl.ds((group % 2) * 16, 16), span] = product[
+                            start : start + 16
+                        ]
+                return carry
+
+            lax.fori_loop(0, 4, columns, 0)
+            core_copies[d].start()
 
     for tick in range(STEPS + 1):
         if tick == TWO_TICK:
@@ -382,7 +448,7 @@
         for _ in range(A_TICKS[tick]):
             waiting.pop(0).start()
 
-    result = sums(5, SLOTS, got_z, 16)
+    result = sums(5, SLOTS, got_z)
     for which in range(2):
         side_sum[which] = result[which]
     for which in range(2):
@@ -392,44 +458,7 @@
         part_copies[0][which].start()
     for copy in waiting:
         copy.start()
-
-    for load in loads[3:5]:
-        load.wait()
-    for copy in a_copies:
-        copy.wait_recv()
-
-    core_copies = [
-        remote(
-            w_part.at[d, 1 - core],
-            core_recv.at[d],
-            core_send_sem.at[d],
-            core_recv_sem.at[d],
-            sibling,
-        )
-        for d in range(4)
-    ]
-    order = (1, 2, 3, 0)
-    for d in order:
-        left = cot_all.at[(x + d) % 4]
-
-        def columns(j, carry, d=d, left=left):
-            product = lax.dot_general(
-                left[...].reshape(QROWS, CH),
-                saved_all[j].reshape(QROWS, CH),
-                (((0,), (0,)), ((), ())),
-                preferred_element_type=F32,
-            )
-            span = pl.ds(pl.multiple_of(j * CH, CH), CH)
-            for group in range(8):
-                for half in range(2):
-                    start = (2 * group + half) * 16
-                    w_part[d, half, group // 2, pl.ds((group % 2) * 16, 16), span] = product[
-                        start : start + 16
-                    ]
-            return carry
-
-        lax.fori_loop(0, 4, columns, 0)
-        core_copies[d].start()
+    start_projection()
 
     y_copies = {}
     for d in order:
@@ -586,15 +615,22 @@
         copy.wait_send()
 
 
+def finish(hidden, grad, w, hidden_out, grad_out, w_out):
+    hidden_out[...] = hidden[...]
+    grad_out[...] = grad[...]
+    w_out[...] = w[...]
+
+
 def shards(
     cells_next, node_embed, enc_mix, out_cotangent, decoded_saved, dec_proj, tile_source, tile_codes
 ):
-    my_band = lax.axis_index("band")
-    table = slot_tables(tile_source, my_band)
     hbm = pl.BlockSpec(memory_space=pl.ANY)
     vmem = pl.BlockSpec(memory_space=pltpu.VMEM)
+    smem = pl.BlockSpec(memory_space=pltpu.SMEM)
     dma = pltpu.SemaphoreType.DMA
     scratch = [
+        pltpu.SMEM((8, BLK), jnp.int32),
+        pltpu.VMEM((8, BLK), jnp.int32),
         pltpu.VMEM((TILES, BLK, BLK), jnp.int32),
         pltpu.VMEM((2, 4, 4, BLK, CH), BF),
         pltpu.VMEM((2, 4, 4, BLK, CH), BF),
@@ -603,9 +639,9 @@
         pltpu.VMEM((4 * CH, CH), BF),
         pltpu.VMEM((4 * CH, CH), BF),
         pltpu.VMEM((NODES, CH), BF),
-        pltpu.VMEM((2 * SLOTS + T2, 2, BLK, BLK), BF),
+        pltpu.VMEM((Z_SLOTS + T2, 2, BLK, BLK), BF),
         pltpu.VMEM((SLOTS, 2, BLK, BLK), BF),
-        pltpu.VMEM((2 * SLOTS, 2, BLK, BLK), BF),
+        pltpu.VMEM((Z_SLOTS, 2, BLK, BLK), BF),
         pltpu.VMEM((SLOTS, 2, BLK, BLK), BF),
         pltpu.VMEM((T2, 2, BLK, BLK), BF),
         pltpu.VMEM((2, NODES, SLOTS * BLK), BF),
@@ -626,13 +662,13 @@
         pltpu.VMEM((3, 32, 4 * CH), BF),
         pltpu.VMEM((2, 4, 16, CH), F32),
         pltpu.VMEM((7, 16, CH), F32),
-        dma((8,)),
+        dma((9,)),
         dma((2,)),
         dma((2,)),
-        dma((10,)),
-        dma((10,)),
-        dma((10,)),
-        dma((10,)),
+        dma((8,)),
+        dma((8,)),
+        dma((8,)),
+        dma((8,)),
         dma((8,)),
         dma((8,)),
         dma,
@@ -655,14 +691,14 @@
         dma((3, 2)),
         dma((2,)),
     ]
-    hidden_nodes, node_grad, w_dec_grad = pl.pallas_call(
+    results = pl.pallas_call(
         kernel,
         out_shape=(
             jax.ShapeDtypeStruct((NODES, CH), BF),
             jax.ShapeDtypeStruct((NODES, CH), BF),
             jax.ShapeDtypeStruct((16, CH), F32),
         ),
-        in_specs=[pl.BlockSpec(memory_space=pltpu.SMEM)] + [hbm] * 7,
+        in_specs=[smem] + [hbm] * 7,
         out_specs=(vmem, vmem, vmem),
         scratch_shapes=scratch,
         compiler_params=pltpu.CompilerParams(
@@ -670,7 +706,7 @@
         ),
         name="encode_and_backward",
     )(
-        table,
+        tile_source.T,
         cells_next.reshape(4, 4, BLK, CH),
         node_embed,
         enc_mix,
@@ -679,7 +715,13 @@
         dec_proj,
         tile_codes.reshape(TILES, BLK, BLK),
     )
-    return hidden_nodes, node_grad, w_dec_grad
+    return pl.pallas_call(
+        finish,
+        out_shape=tuple(jax.ShapeDtypeStruct(r.shape, r.dtype) for r in results),
+        in_specs=[vmem] * 3,
+        out_specs=(vmem, vmem, vmem),
+        name="finish",
+    )(*results)
 
 
 def solution(mesh):

time: 126 us -> 114 us (0.905); the launches traced: 124 us -> 114 us
  local copies, waits for them, and re-layouts: 6.08 us -> 0 us
  Pallas kernels: 116 us -> 113 us
    unnamed x4 -> x0, local copies, waits for them, and re-layouts: 5.26 us -> none
    pallas_call x1, Pallas kernels: 116 us -> 111 us  [shards(): pl.pallas_call(kernel, out_shape=(jax.ShapeDtypeStruct((NODES, CH), BF),...]
    pallas_call x0 -> x1, Pallas kernels: none -> 1.68 us  [shards(): pl.pallas_call(finish, out_shape=tuple((jax.ShapeDtypeStruct(r.shape, r.d...]
where the time goes in v4:
time: 114 us
  Pallas kernels  113 us (99%)
    pallas_call x1, Pallas kernels, shards(): pl.pallas_call(kernel, out_shape=(jax.ShapeDtypeStruct((NODES, CH), BF),...  111 us

profile of v4, /device:TPU:32, one launch (start us, length us, event | category | flops | bytes accessed | tf_op | source)
XLA Modules:
  0.0 113.6 jit_solution(17964613199077098996)
XLA Ops:
  0.6 111.3 %encode_and_backward.1 = (bf16[256,256]{1,0:T(8,128)(2,1)}, bf16[256,256]{1,0:T(8,128)(2,1)}, f32[16,256]{1,0:T(8,128)}) custom-call(s32[16,128]{1,0:T(8,128)} %bitcast.9, bf16[4,4,128,256]{3,2,1,0:T(8,128)(2,1)} %bitcast.6, bf16[256,256]{1,0:T(8,128)(2,1)} %embed_hbm.1, bf16[1024,256]{1,0:T(8,128)(2,1)} %mix_hbm.1, bf16[4,4,128,256]{3,2,1,0:T(8,128)(2,1)} %bitcast.7, ...), custom_call_target="tpu_custom_call" | custom-call | tf_op jit(solution)/shard_map/encode_and_backward/pallas_call | solution.py:694
  112.0 1.7 %finish.1 = (bf16[256,256]{1,0:T(8,128)(2,1)}, bf16[256,256]{1,0:T(8,128)(2,1)}, f32[16,256]{1,0:T(8,128)}) custom-call(bf16[256,256]{1,0:T(8,128)(2,1)} %get-tuple-element.6.hidden, bf16[256,256]{1,0:T(8,128)(2,1)} %get-tuple-element.7.grad, f32[16,256]{1,0:T(8,128)} %get-tuple-element.8.w), custom_call_target="tpu_custom_call" | custom-call | tf_op jit(solution)/shard_map/finish/pallas_call | solution.py:718

commit v5 on v4

--- a/solution.py
+++ b/solution.py
@@ -13,6 +13,7 @@
 SLOTS = 16
 T2 = 8
 CH = 256
+COLS = 512
 ROWS = 2048
 QROWS = 512
 NODES = 256
@@ -85,6 +86,11 @@
     y_recv,
     x_send,
     x_recv,
+    wide_own,
+    wide_send,
+    wide_recv,
+    last_send,
+    last_recv,
     z_send,
     z_recv,
     load_sem,
@@ -106,6 +112,10 @@
     y_recv_sem,
     x_send_sem,
     x_recv_sem,
+    wide_send_sem,
+    wide_recv_sem,
+    last_send_sem,
+    last_recv_sem,
     z_send_sem,
     z_recv_sem,
     beyond_send_sem,
@@ -204,12 +214,6 @@
         ranks = tuple(rank + jnp.where(hit, 1, 0) for rank, hit in zip(ranks, hits))
         return rows, ranks
 
-    zero = jnp.int32(0)
-    table_rows[...] = lax.fori_loop(
-        0, TILES, place, (jnp.zeros((8, BLK), jnp.int32), (zero,) * 7)
-    )[0]
-    table_load = pltpu.make_async_copy(table_rows, table, load_sem.at[8])
-
     def pack(row, count, dest, base):
         def one(s, carry):
             item = table[row, s]
@@ -241,6 +245,12 @@
                 )
     waiting = list(a_copies)
 
+    zero = jnp.int32(0)
+    table_rows[...] = lax.fori_loop(
+        0, TILES, place, (jnp.zeros((8, BLK), jnp.int32), (zero,) * 7)
+    )[0]
+    table_load = pltpu.make_async_copy(table_rows, table, load_sem.at[8])
+
     pl.semaphore_wait(barrier, len(partners))
     for _ in range(A_FIRST):
         waiting.pop(0).start()
@@ -460,13 +470,63 @@
         copy.start()
     start_projection()
 
+    def agg_copy(d, which):
+        return remote(
+            agg_all.at[q, which],
+            agg_all.at[q, which],
+            agg_send_sem.at[d - 1, which],
+            agg_recv_sem.at[d - 1, which],
+            (band, (q + d) % 4),
+        )
+
+    def hop_copy(which):
+        block = (q + 2) % 4
+        return remote(
+            agg_all.at[block, which],
+            agg_all.at[block, which],
+            hop_send_sem.at[which],
+            agg_recv_sem.at[2 * (q - 1), which],
+            (band, 3 * (q - 1)),
+        )
+
+    middle = (q == 1) | (q == 2)
+
+    def far(d):
+        return ((q == 0) & (d == 3)) | ((q == 3) & (d == 1))
+
+    for which in range(2):
+        total = own_sum[which]
+        for g in range(2):
+            part_copies[g][which].wait_recv()
+            total = total + part_recv[g, which].astype(F32)
+        agg_all[q, which] = (total * SCALE).astype(BF)
+        for d in (2, 1, 3):
+
+            @pl.when(jnp.logical_not(far(d)))
+            def _(d=d, which=which):
+                agg_copy(d, which).start()
+
     y_copies = {}
+    wide_copies = {}
     for d in order:
         core_copies[d].wait_recv()
         for yy in range(4):
             total = w_part[d, core, yy] + core_recv[d, yy]
-            y_own[d, yy] = total
-            y_send[d, yy] = total.astype(BF)
+            y_own[d, yy] = total[:, :COLS]
+            y_send[d, yy] = total[:, :COLS].astype(BF)
+            if d > 0:
+                wide_send[d - 1, yy] = total[:, COLS:].astype(BF)
+            else:
+                wide_own[yy] = total[:, COLS:]
+        if d > 0:
+            wide_copies[d] = remote(
+                wide_send.at[d - 1],
+                wide_recv.at[d - 1],
+                wide_send_sem.at[d - 1],
+                wide_recv_sem.at[d - 1],
+                along_x[d - 1],
+            )
+            wide_copies[d].start()
         for e in range(1, 4):
             y_copies[d, e] = remote(
                 y_send.at[d, (y + e) % 4],
@@ -477,42 +537,24 @@
             )
             y_copies[d, e].start()
 
-    def agg_copy(d, which):
-        return remote(
-            agg_all.at[q, which],
-            agg_all.at[q, which],
-            agg_send_sem.at[d - 1, which],
-            agg_recv_sem.at[d - 1, which],
-            (band, (q + d) % 4),
-        )
-
-    def hop_copy(which):
-        block = (q + 2) % 4
-        return remote(
-            agg_all.at[block, which],
-            agg_all.at[block, which],
-            hop_send_sem.at[which],
-            agg_recv_sem.at[2 * (q - 1), which],
-            (band, 3 * (q - 1)),
-        )
-
-    middle = (q == 1) | (q == 2)
-
-    def far(d):
-        return ((q == 0) & (d == 3)) | ((q == 3) & (d == 1))
-
-    for which in range(2):
-        total = own_sum[which]
-        for g in range(2):
-            part_copies[g][which].wait_recv()
-            total = total + part_recv[g, which].astype(F32)
-        agg_all[q, which] = (total * SCALE).astype(BF)
-        for d in (2, 1, 3):
-
-            @pl.when(jnp.logical_not(far(d)))
-            def _(d=d, which=which):
-                agg_copy(d, which).start()
-
+    last_copies = {}
+    for d in range(1, 4):
+        wide_copies[d].wait_recv()
+    for yy in range(4):
+        total = wide_own[yy]
+        for d in range(1, 4):
+            total = total + wide_recv[d - 1, yy].astype(F32)
+        wide_own[yy] = total
+        last_send[yy] = total.astype(BF)
+    for e in range(1, 4):
+        last_copies[e] = remote(
+            last_send.at[(y + e) % 4],
+            last_recv.at[e - 1],
+            last_send_sem.at[e - 1],
+            last_recv_sem.at[e - 1],
+            along_y[e - 1],
+        )
+        last_copies[e].start()
     x_copies = {}
     for d in order:
         total = y_own[d, y]
@@ -536,12 +578,18 @@
         def _(which=which):
             hop_copy(which).start()
 
+    other = wide_own[y]
     for d in range(1, 4):
         x_copies[d].wait_recv()
         total = total + x_recv[d - 1].astype(F32)
+        last_copies[d].wait_recv()
+        other = other + last_recv[d - 1].astype(F32)
     for hh in range(2):
-        for qq in range(4):
-            z_send[hh, qq] = total[hh * 16 : hh * 16 + 16, qq * CH : qq * CH + CH]
+        rows = slice(hh * 16, hh * 16 + 16)
+        for qq in range(2):
+            span = slice(qq * CH, qq * CH + CH)
+            z_send[hh, qq] = total[rows, span]
+            z_send[hh, qq + 2] = other[rows, span]
     z_copies = []
     for hd in range(2):
         for qd in range(4):
@@ -611,7 +659,9 @@
 
     ends = shares + a_copies + beyond_copies + part_copies[0] + part_copies[1]
     ends = ends + core_copies + z_copies
-    for copy in ends + list(y_copies.values()) + list(x_copies.values()):
+    for some in (y_copies, x_copies, wide_copies, last_copies):
+        ends = ends + list(some.values())
+    for copy in ends:
         copy.wait_send()
 
 
@@ -655,11 +705,16 @@
         pltpu.VMEM((4, 2, NODES, CH), BF),
         pltpu.VMEM((4, 2, 4, 32, 4 * CH), F32),
         pltpu.VMEM((4, 4, 32, 4 * CH), F32),
-        pltpu.VMEM((4, 4, 32, 4 * CH), F32),
-        pltpu.VMEM((4, 4, 32, 4 * CH), BF),
-        pltpu.VMEM((4, 3, 32, 4 * CH), BF),
-        pltpu.VMEM((3, 32, 4 * CH), BF),
-        pltpu.VMEM((3, 32, 4 * CH), BF),
+        pltpu.VMEM((4, 4, 32, COLS), F32),
+        pltpu.VMEM((4, 4, 32, COLS), BF),
+        pltpu.VMEM((4, 3, 32, COLS), BF),
+        pltpu.VMEM((3, 32, COLS), BF),
+        pltpu.VMEM((3, 32, COLS), BF),
+        pltpu.VMEM((4, 32, COLS), F32),
+        pltpu.VMEM((3, 4, 32, COLS), BF),
+        pltpu.VMEM((3, 4, 32, COLS), BF),
+        pltpu.VMEM((4, 32, COLS), BF),
+        pltpu.VMEM((3, 32, COLS), BF),
         pltpu.VMEM((2, 4, 16, CH), F32),
         pltpu.VMEM((7, 16, CH), F32),
         dma((9,)),
@@ -679,6 +734,10 @@
         dma((4,)),
         dma((4, 3)),
         dma((4, 3)),
+        dma((3,)),
+        dma((3,)),
+        dma((3,)),
+        dma((3,)),
         dma((3,)),
         dma((3,)),
         dma((7,)),

time: 114 us -> 111 us (0.974)
  Pallas kernels: 113 us -> 111 us
    pallas_call x1, Pallas kernels: 111 us -> 109 us  [shards(): pl.pallas_call(kernel, out_shape=(jax.ShapeDtypeStruct((NODES, CH), BF),...]
where the time goes in v5:
time: 111 us
  Pallas kernels  111 us (100%)
    pallas_call x1, Pallas kernels, shards(): pl.pallas_call(kernel, out_shape=(jax.ShapeDtypeStruct((NODES, CH), BF),...  109 us

profile of v5, /device:TPU:32, one launch (start us, length us, event | category | flops | bytes accessed | tf_op | source)
XLA Modules:
  0.0 111.2 jit_solution(14012272136496499531)
XLA Ops:
  0.6 108.9 %encode_and_backward.1 = (bf16[256,256]{1,0:T(8,128)(2,1)}, bf16[256,256]{1,0:T(8,128)(2,1)}, f32[16,256]{1,0:T(8,128)}) custom-call(s32[16,128]{1,0:T(8,128)} %bitcast.9, bf16[4,4,128,256]{3,2,1,0:T(8,128)(2,1)} %bitcast.6, bf16[256,256]{1,0:T(8,128)(2,1)} %embed_hbm.1, bf16[1024,256]{1,0:T(8,128)(2,1)} %mix_hbm.1, bf16[4,4,128,256]{3,2,1,0:T(8,128)(2,1)} %bitcast.7, ...), custom_call_target="tpu_custom_call" | custom-call | tf_op jit(solution)/shard_map/encode_and_backward/pallas_call | solution.py:753
  109.6 1.7 %finish.1 = (bf16[256,256]{1,0:T(8,128)(2,1)}, bf16[256,256]{1,0:T(8,128)(2,1)}, f32[16,256]{1,0:T(8,128)}) custom-call(bf16[256,256]{1,0:T(8,128)(2,1)} %get-tuple-element.6.hidden, bf16[256,256]{1,0:T(8,128)(2,1)} %get-tuple-element.7.grad, f32[16,256]{1,0:T(8,128)} %get-tuple-element.8.w), custom_call_target="tpu_custom_call" | custom-call | tf_op jit(solution)/shard_map/finish/pallas_call | solution.py:777
